TPU v7x, 32 devices: a whole 2x2x4 slice. The times are simulated.
32 devices in a mesh: dp: 8 (over y, x, core), tp: 4 (over z).
Axes of the slice: x: 2, y: 2, z: 4, core: 2. Of those that a mesh axis runs over, the one named last changes fastest.
Arguments:
- tokens: bfloat16 [128, 8192], P('tp', 'dp'), may hold values from -6 to 6
- targets: bfloat16 [128, 8192], P('tp', 'dp'), may hold values from -6 to 6
- gate_weight: bfloat16 [8192, 16384], P('dp', 'tp'), may hold values from -0.0625 to 0.0625
- up_weight: bfloat16 [8192, 16384], P('dp', 'tp'), may hold values from -0.0625 to 0.0625
- down_weight: bfloat16 [16384, 8192], P('tp', 'dp'), may hold values from -0.046875 to 0.046875
- direction_gate: bfloat16 [8192, 16384], P('dp', 'tp'), may hold values from -36 to 36
- direction_up: bfloat16 [8192, 16384], P('dp', 'tp'), may hold values from -36 to 36
- direction_down: bfloat16 [16384, 8192], P('tp', 'dp'), may hold values from -36 to 36
- previous_gate: bfloat16 [8192, 16384], P('dp', 'tp'), may hold values from -36 to 36
- previous_up: bfloat16 [8192, 16384], P('dp', 'tp'), may hold values from -36 to 36
- previous_down: bfloat16 [16384, 8192], P('tp', 'dp'), may hold values from -36 to 36
- beta_prev: float32 [1], replicated, may hold values from 1 to 4
Outputs:
- next_gate: bfloat16 [8192, 16384], P('dp', 'tp')
- next_up: bfloat16 [8192, 16384], P('dp', 'tp')
- next_down: bfloat16 [16384, 8192], P('tp', 'dp')
- coefficients: float32 [2], replicated
All inputs are finite; a program needn't handle non-finite values.
Results may differ from a plain program's by a relative error of at most 0.015.
Values may be sent and summed in bfloat16 or wider, within the bound.
A program may use at most 256 MiB of HBM per device.

v0:
```python
import functools

import jax
import jax.numpy as jnp
from jax import lax
from jax.experimental import pallas as pl
from jax.experimental.pallas import tpu as pltpu
from jax.sharding import PartitionSpec as P

MESH = pl.DeviceIdType.MESH
VMEM = pltpu.VMEM
DMA = pltpu.SemaphoreType.DMA
F32 = jnp.float32
BF16 = jnp.bfloat16
LIMIT = 56 * 1024 * 1024


def tile_of(size, most):
    tile = min(size, most)
    while size % tile:
        tile //= 2
    return tile


def greet(targets):
    barrier = pltpu.get_barrier_semaphore()
    for target in targets:
        pl.semaphore_signal(barrier, inc=1, device_id=target, device_id_type=MESH)
    pl.semaphore_wait(barrier, len(targets))


def send(src, dst, send_sem, recv_sem, target):
    copy = pltpu.make_async_remote_copy(
        src_ref=src, dst_ref=dst, send_sem=send_sem, recv_sem=recv_sem, device_id=target, device_id_type=MESH
    )
    copy.start()
    return copy


def by_columns(width, body):
    step = tile_of(width, 512)

    @pl.loop(0, width // step)
    def _(i):
        body(pl.ds(pl.multiple_of(i * step, step), step))


def forward_rows(parts, keeps, cols):
    gate_sum, up_sum, gate_dir, up_dir = parts
    for keep, part in zip(keeps, parts):
        keep[:, cols] = part
    logistic = jax.nn.sigmoid(gate_sum)
    activation = gate_sum * logistic
    gate_slope = logistic * (1.0 + gate_sum * (1.0 - logistic))
    hidden = activation * up_sum
    hidden_dir = gate_slope * up_sum * gate_dir + activation * up_dir
    return hidden, hidden_dir


def backward_rows(parts, keeps, cols):
    grad_hidden, grad_hidden_dir = parts
    gate_sum, up_sum, gate_dir, up_dir = (keep[:, cols] for keep in keeps)
    logistic = jax.nn.sigmoid(gate_sum)
    activation = gate_sum * logistic
    gate_slope = logistic * (1.0 + gate_sum * (1.0 - logistic))
    gate_curve = logistic * (1.0 - logistic) * (2.0 + gate_sum * (1.0 - 2.0 * logistic))
    grad_gate = (
        grad_hidden_dir * up_sum * gate_slope
        + grad_hidden * up_dir * gate_slope
        + grad_hidden * up_sum * gate_curve * gate_dir
    )
    grad_up = grad_hidden_dir * activation + grad_hidden * gate_slope * gate_dir
    return grad_gate, grad_up


def width_kernel(n, kinds, rows_of, keeps_in, *refs):
    x = refs[0]
    if keeps_in:
        keeps, out = refs[1:5], refs[5]
    else:
        out, keeps = refs[1], refs[2:6]
    mate_in, paired, far_in, full, s1, r1, s2, r2, s3, r3, s4, r4, local = refs[6:]
    chips = n // 2
    width = x.shape[-1]
    me = lax.axis_index("dp")
    chip, core = lax.div(me, 2), lax.rem(me, 2)
    mate = {"dp": me + 1 - 2 * core}
    afar = [{"dp": lax.rem(chip + s, chips) * 2 + core} for s in range(1, chips)]
    greet([mate] + afar)

    order = list(range(1, chips)) + [0]
    spot = [lax.rem(chip + s, chips) for s in range(chips)]
    source = [lax.rem(chip + chips - s, chips) for s in range(chips)]
    first = {
        s: send(x.at[:, spot[s], 1 - core], mate_in.at[:, spot[s]], s1.at[s], r1.at[s], mate)
        for s in order
    }
    second = {}
    for s in order:
        first[s].wait_recv()

        def pair(cols, s=s):
            for kind in range(kinds):
                paired[kind, spot[s], :, cols] = (
                    x[kind, spot[s], core, :, cols].astype(F32)
                    + mate_in[kind, spot[s], :, cols].astype(F32)
                ).astype(BF16)

        by_columns(width, pair)
        if s:
            second[s] = send(
                paired.at[:, spot[s]], far_in.at[:, chip], s2.at[s], r2.at[s], afar[s - 1]
            )
    for s in range(1, chips):
        second[s].wait_recv()

    def finish(cols):
        parts = []
        for kind in range(kinds):
            total = paired[kind, chip, :, cols].astype(F32)
            for s in range(1, chips):
                total = total + far_in[kind, source[s], :, cols].astype(F32)
            parts.append(total)
        one, two = rows_of(parts, keeps, cols)
        full[0, me, :, cols] = one.astype(BF16)
        full[1, me, :, cols] = two.astype(BF16)

    by_columns(width, finish)

    mine = full.at[:, me]
    third = [send(mine, mine, s3.at[s], r3.at[s], afar[s - 1]) for s in range(1, chips)]
    fourth = [send(mine, mine, s4.at[0], r4.at[0], mate)]
    stores = [pltpu.make_async_copy(mine, out.at[:, me], local.at[0])]
    stores[0].start()
    for s in range(1, chips):
        third[s - 1].wait_recv()
        at = source[s] * 2 + core
        fourth.append(send(full.at[:, at], full.at[:, at], s4.at[s], r4.at[s], mate))
        store = pltpu.make_async_copy(full.at[:, at], out.at[:, at], local.at[s])
        store.start()
        stores.append(store)
    for s in range(chips):
        fourth[s].wait_recv()
        at = source[s] * 2 + 1 - core
        store = pltpu.make_async_copy(full.at[:, at], out.at[:, at], local.at[chips + s])
        store.start()
        stores.append(store)
    for copy in list(first.values()) + list(second.values()) + third + fourth:
        copy.wait_send()
    for store in stores:
        store.wait()


def width_exchange(n, x, keeps, rows_of, collective_id):
    kinds, rows, width = x.shape
    share, chips = rows // n, n // 2
    keeps_in = keeps is not None
    x = x.reshape(kinds, chips, 2, share, width)
    vmem, anywhere = pl.BlockSpec(memory_space=VMEM), pl.BlockSpec(memory_space=pl.ANY)
    out_shape = [jax.ShapeDtypeStruct((2, n, share, width), BF16)]
    out_specs = [anywhere]
    if not keeps_in:
        out_shape += [jax.ShapeDtypeStruct((share, width), F32)] * 4
        out_specs += [vmem] * 4
    slots = VMEM((kinds, chips, share, width), BF16)
    sems = DMA((chips,))
    result = pl.pallas_call(
        functools.partial(width_kernel, n, kinds, rows_of, keeps_in),
        out_shape=out_shape,
        in_specs=[vmem] * (5 if keeps_in else 1),
        out_specs=out_specs,
        scratch_shapes=[slots, slots, slots, VMEM((2, n, share, width), BF16)]
        + [sems] * 8
        + [DMA((n,))],
        compiler_params=pltpu.CompilerParams(
            collective_id=collective_id, has_side_effects=True, vmem_limit_bytes=LIMIT
        ),
    )(x, *(keeps or ()))
    return result[0].reshape(2, rows, width), tuple(result[1:])


def ring_of(t):
    me = lax.axis_index("tp")
    return me, [lax.rem(me + s, t) for s in range(1, t)], [lax.rem(me + t - s, t) for s in range(1, t)]


def tokens_kernel(t, x, out, full, ssem, rsem, local):
    me, spots, sources = ring_of(t)
    greet([{"tp": spot} for spot in spots])
    copies = [
        send(x, full.at[me], ssem.at[i], rsem.at[i], {"tp": spot}) for i, spot in enumerate(spots)
    ]
    stores = [pltpu.make_async_copy(x, out.at[me], local.at[t - 1])]
    stores[0].start()
    for i, copy in enumerate(copies):
        copy.wait_recv()
        store = pltpu.make_async_copy(full.at[sources[i]], out.at[sources[i]], local.at[i])
        store.start()
        stores.append(store)
    for copy in copies:
        copy.wait_send()
    for store in stores:
        store.wait()


def tokens_exchange(t, x):
    share, width = x.shape
    out = pl.pallas_call(
        functools.partial(tokens_kernel, t),
        out_shape=jax.ShapeDtypeStruct((t, share, width), BF16),
        in_specs=[pl.BlockSpec(memory_space=VMEM)],
        out_specs=pl.BlockSpec(memory_space=pl.ANY),
        scratch_shapes=[VMEM((t, share, width), BF16), DMA((t - 1,)), DMA((t - 1,)), DMA((t,))],
        compiler_params=pltpu.CompilerParams(
            collective_id=1, has_side_effects=True, vmem_limit_bytes=LIMIT
        ),
    )(x)
    return out.reshape(t * share, width)


def output_kernel(t, x, targets, out, far_in, full, s1, r1, s2, r2, local):
    me, spots, sources = ring_of(t)
    share, width = targets.shape
    rows = t * share
    greet([{"tp": spot} for spot in spots])
    first = [
        send(x.at[:, spot], far_in.at[:, me], s1.at[i], r1.at[i], {"tp": spot})
        for i, spot in enumerate(spots)
    ]
    for copy in first:
        copy.wait_recv()

    def finish(cols):
        parts = []
        for kind in range(2):
            total = x[kind, me, :, cols].astype(F32)
            for at in sources:
                total = total + far_in[kind, at, :, cols].astype(F32)
            parts.append(total)
        full[0, me, :, cols] = ((parts[0] - targets[:, cols].astype(F32)) / rows).astype(BF16)
        full[1, me, :, cols] = (parts[1] / rows).astype(BF16)

    by_columns(width, finish)
    mine = full.at[:, me]
    second = [
        send(mine, mine, s2.at[i], r2.at[i], {"tp": spot}) for i, spot in enumerate(spots)
    ]
    stores = [pltpu.make_async_copy(mine, out.at[:, me], local.at[t - 1])]
    stores[0].start()
    for i, copy in enumerate(second):
        copy.wait_recv()
        at = sources[i]
        store = pltpu.make_async_copy(full.at[:, at], out.at[:, at], local.at[i])
        store.start()
        stores.append(store)
    for copy in first + second:
        copy.wait_send()
    for store in stores:
        store.wait()


def output_exchange(t, x, targets):
    _, rows, width = x.shape
    share = rows // t
    vmem = pl.BlockSpec(memory_space=VMEM)
    slots = VMEM((2, t, share, width), BF16)
    out = pl.pallas_call(
        functools.partial(output_kernel, t),
        out_shape=jax.ShapeDtypeStruct((2, t, share, width), BF16),
        in_specs=[vmem, vmem],
        out_specs=pl.BlockSpec(memory_space=pl.ANY),
        scratch_shapes=[slots, slots] + [DMA((t - 1,))] * 4 + [DMA((t,))],
        compiler_params=pltpu.CompilerParams(
            collective_id=2, has_side_effects=True, vmem_limit_bytes=LIMIT
        ),
    )(x.reshape(2, t, share, width), targets)
    return out.reshape(2, rows, width)


def totals_kernel(n, t, entries, x, beta_prev, out, dp_in, sums, tp_in, s1, r1, s2, r2, local):
    dp, tp = lax.axis_index("dp"), lax.axis_index("tp")
    dp_spots = [lax.rem(dp + s, n) for s in range(1, n)]
    tp_spots = [lax.rem(tp + s, t) for s in range(1, t)]
    greet([{"dp": spot} for spot in dp_spots] + [{"tp": spot} for spot in tp_spots])
    first = [
        send(x, dp_in.at[dp], s1.at[i], r1.at[i], {"dp": spot}) for i, spot in enumerate(dp_spots)
    ]
    dp_in[dp] = x[...]
    for copy in first:
        copy.wait_recv()
    total = dp_in[0]
    for at in range(1, n):
        total = total + dp_in[at]
    sums[...] = total
    tp_in[tp] = total
    second = [
        send(sums, tp_in.at[tp], s2.at[i], r2.at[i], {"tp": spot})
        for i, spot in enumerate(tp_spots)
    ]
    for copy in second:
        copy.wait_recv()
    total = tp_in[0]
    for at in range(1, t):
        total = total + tp_in[at]
    image_image, image_along, image_before = total[0:1], total[1:2], total[2:3]
    along_along, along_before, before_before = total[3:4], total[4:5], total[5:6]
    beta_old = beta_prev[0]
    alpha_coef = image_along / entries
    square = (
        image_image
        - 2.0 * alpha_coef * image_along
        - 2.0 * beta_old * image_before
        + alpha_coef * alpha_coef * along_along
        + 2.0 * alpha_coef * beta_old * along_before
        + beta_old * beta_old * before_before
    )
    beta_coef = jnp.sqrt(square / entries + 1e-06)
    inverse = 1.0 / beta_coef
    out[0:1] = alpha_coef
    out[1:2] = beta_coef
    out[2:3] = inverse
    out[3:4] = alpha_coef * inverse
    out[4:5] = beta_old * inverse
    out[5:8] = jnp.zeros((3, total.shape[1]), F32)
    for copy in first + second:
        copy.wait_send()


def totals_exchange(n, t, entries, x, beta_prev):
    vmem = pl.BlockSpec(memory_space=VMEM)
    rows, lanes = x.shape
    return pl.pallas_call(
        functools.partial(totals_kernel, n, t, entries),
        out_shape=jax.ShapeDtypeStruct((rows, lanes), F32),
        in_specs=[vmem, pl.BlockSpec(memory_space=pltpu.SMEM)],
        out_specs=vmem,
        scratch_shapes=[
            VMEM((n, rows, lanes), F32),
            VMEM((rows, lanes), F32),
            VMEM((t, rows, lanes), F32),
            DMA((n - 1,)),
            DMA((n - 1,)),
            DMA((t - 1,)),
            DMA((t - 1,)),
            DMA((1,)),
        ],
        compiler_params=pltpu.CompilerParams(collective_id=3, has_side_effects=True),
    )(x, beta_prev)


def squares(along_ref, before_ref, norms):
    rows, width = along_ref.shape
    step = tile_of(rows, 32)

    def body(i, sums):
        at = pl.ds(pl.multiple_of(i * step, step), step)
        along = along_ref[at, :].astype(F32)
        before = before_ref[at, :].astype(F32)
        products = (along * along, along * before, before * before)
        return tuple(
            have + product.reshape(step // 8, 8, width).sum(axis=0)
            for have, product in zip(sums, products)
        )

    zero = jnp.zeros((8, width), F32)
    sums = lax.fori_loop(0, rows // step, body, (zero, zero, zero))
    for kind in range(3):
        norms[kind] += sums[kind]


def dot(one, two):
    return jnp.dot(one, two, preferred_element_type=F32)


def front_kernel(tokens, gate, up, along_gate, along_up, before_gate, before_up, x, before, norms):
    @pl.when(pl.program_id(0) == 0)
    def _():
        norms[...] = jnp.zeros_like(norms)

    rows = tokens[...]
    for kind, ref in enumerate((gate, up, along_gate, along_up)):
        x[kind] = dot(rows, ref[...]).astype(BF16)
    for kind, ref in enumerate((before_gate, before_up)):
        before[kind] = dot(rows, ref[...]).astype(BF16)
    squares(along_gate, before_gate, norms)
    squares(along_up, before_up, norms)


def front_products(tokens, *matrices):
    rows, depth = tokens.shape
    width = matrices[0].shape[1]
    tile = tile_of(width, 512)
    return pl.pallas_call(
        front_kernel,
        grid=(width // tile,),
        out_shape=(
            jax.ShapeDtypeStruct((4, rows, width), BF16),
            jax.ShapeDtypeStruct((2, rows, width), BF16),
            jax.ShapeDtypeStruct((3, 8, tile), F32),
        ),
        in_specs=[pl.BlockSpec((rows, depth), lambda i: (0, 0))]
        + [pl.BlockSpec((depth, tile), lambda i: (0, i))] * 6,
        out_specs=(
            pl.BlockSpec((4, rows, tile), lambda i: (0, 0, i)),
            pl.BlockSpec((2, rows, tile), lambda i: (0, 0, i)),
            pl.BlockSpec((3, 8, tile), lambda i: (0, 0, 0)),
        ),
        compiler_params=pltpu.CompilerParams(vmem_limit_bytes=LIMIT),
    )(tokens, *matrices)


def middle_kernel(units, down, along, before, weighted, moved, was, norms):
    @pl.when(pl.program_id(0) == 0)
    def _():
        for ref in (weighted, moved, was, norms):
            ref[...] = jnp.zeros_like(ref)

    rows = units[...]
    weighted[...] += dot(rows, down[...])
    moved[...] += dot(rows, along[...])
    was[...] += dot(rows, before[...])
    squares(along, before, norms)


def middle_products(units, down, along, before):
    rows, depth = units.shape
    width = down.shape[1]
    tile = tile_of(depth, 512)
    whole = pl.BlockSpec((rows, width), lambda i: (0, 0))
    return pl.pallas_call(
        middle_kernel,
        grid=(depth // tile,),
        out_shape=[jax.ShapeDtypeStruct((rows, width), F32)] * 3
        + [jax.ShapeDtypeStruct((3, 8, width), F32)],
        in_specs=[pl.BlockSpec((rows, tile), lambda i: (0, i))]
        + [pl.BlockSpec((tile, width), lambda i: (i, 0))] * 3,
        out_specs=[whole] * 3 + [pl.BlockSpec((3, 8, width), lambda i: (0, 0, 0))],
        compiler_params=pltpu.CompilerParams(vmem_limit_bytes=LIMIT),
    )(units, down, along, before)


def against(one, two):
    return lax.dot_general(one, two, (((1,), (1,)), ((), ())), preferred_element_type=F32)


def transposed(one, two):
    return lax.dot_general(one, two, (((0,), (0,)), ((), ())), preferred_element_type=F32)


def back_kernel(grads, down, along, x):
    rows = grads.shape[0] // 2
    weighted = against(grads[...], down[...])
    moved = against(grads[:rows, :], along[...])
    x[0] = weighted[:rows].astype(BF16)
    x[1] = (weighted[rows:] + moved).astype(BF16)


def back_products(grads, down, along):
    rows, depth = grads.shape
    width = down.shape[0]
    tile = tile_of(width, 512)
    return pl.pallas_call(
        back_kernel,
        grid=(width // tile,),
        out_shape=jax.ShapeDtypeStruct((2, rows // 2, width), BF16),
        in_specs=[pl.BlockSpec((rows, depth), lambda i: (0, 0))]
        + [pl.BlockSpec((tile, depth), lambda i: (i, 0))] * 2,
        out_specs=pl.BlockSpec((2, rows // 2, tile), lambda i: (0, 0, i)),
        compiler_params=pltpu.CompilerParams(vmem_limit_bytes=LIMIT),
    )(grads, down, along)


def next_kernel(count, scales, *refs):
    one, rest = refs[0], refs[1:]
    twos, alongs, befores, outs = (rest[i * count : (i + 1) * count] for i in range(4))
    inverse, alpha, beta = scales[2, 0], scales[3, 0], scales[4, 0]
    for two, along, before, out in zip(twos, alongs, befores, outs):
        image = transposed(one[...], two[...])
        out[...] = (
            image * inverse - along[...].astype(F32) * alpha - before[...].astype(F32) * beta
        ).astype(BF16)


def next_parts(scales, one, twos, alongs, befores):
    count = len(twos)
    rows, height = one.shape
    width = twos[0].shape[1]
    tile = tile_of(height, max(128, (1 << 20) // (width * count)))
    block = pl.BlockSpec((tile, width), lambda i: (i, 0))
    return pl.pallas_call(
        functools.partial(next_kernel, count),
        grid=(height // tile,),
        out_shape=[jax.ShapeDtypeStruct((height, width), BF16)] * count,
        in_specs=[pl.BlockSpec(memory_space=pltpu.SMEM), pl.BlockSpec((rows, tile), lambda i: (0, i))]
        + [pl.BlockSpec((rows, width), lambda i: (0, 0))] * count
        + [block] * (2 * count),
        out_specs=[block] * count,
        compiler_params=pltpu.CompilerParams(vmem_limit_bytes=LIMIT),
    )(scales, one, *twos, *alongs, *befores)


def on_device(
    n,
    t,
    tokens,
    targets,
    gate_weight,
    up_weight,
    down_weight,
    direction_gate,
    direction_up,
    direction_down,
    previous_gate,
    previous_up,
    previous_down,
    beta_prev,
):
    everyone = tokens_exchange(t, tokens)
    rows = everyone.shape[0]
    x, before, norms = front_products(
        everyone, gate_weight, up_weight, direction_gate, direction_up, previous_gate, previous_up
    )
    units, keeps = width_exchange(n, x, None, forward_rows, 4)
    units = units.reshape(2 * rows, -1)
    weighted, moved, was, down_norms = middle_products(
        units, down_weight, direction_down, previous_down
    )
    outputs = jnp.stack([weighted[:rows], weighted[rows:] + moved[:rows]]).astype(BF16)
    grads = output_exchange(t, outputs, targets)
    grads = grads.reshape(2 * rows, -1)
    y = back_products(grads, down_weight, direction_down)
    dirs, _ = width_exchange(n, y, keeps, backward_rows, 5)

    swapped = jnp.concatenate([units[rows:], units[:rows]])
    gram = against(dirs[0], dirs[0]) + against(dirs[1], dirs[1])
    image_image = jnp.sum(against(everyone, everyone) * gram) + jnp.sum(
        against(swapped, swapped) * against(grads, grads)
    )
    swapped_moved = jnp.concatenate([moved[rows:], moved[:rows]])
    swapped_was = jnp.concatenate([was[rows:], was[:rows]])
    wide = dirs.astype(F32)
    tall = grads.astype(F32)
    image_along = jnp.sum(wide * x[2:].astype(F32)) + jnp.sum(tall * swapped_moved)
    image_before = jnp.sum(wide * before.astype(F32)) + jnp.sum(tall * swapped_was)
    own = jnp.sum(norms, axis=(1, 2)) + jnp.sum(down_norms, axis=(1, 2))
    sums = jnp.concatenate([jnp.stack([image_image, image_along, image_before]), own])
    sums = jnp.broadcast_to(jnp.pad(sums, (0, 2))[:, None], (8, 128))
    entries = float(n * t * (gate_weight.size + up_weight.size + down_weight.size))
    scales = totals_exchange(n, t, entries, sums, beta_prev)
    next_gate, next_up = next_parts(
        scales,
        everyone,
        (dirs[0], dirs[1]),
        (direction_gate, direction_up),
        (previous_gate, previous_up),
    )
    (next_down,) = next_parts(scales, swapped, (grads,), (direction_down,), (previous_down,))
    return (next_gate, next_up, next_down, scales[:2, 0])


def solution(mesh):
    wide, tall = P("dp", "tp"), P("tp", "dp")
    in_specs = (tall, tall, wide, wide, tall, wide, wide, tall, wide, wide, tall, P())
    return jax.shard_map(
        functools.partial(on_device, mesh.shape["dp"], mesh.shape["tp"]),
        mesh=mesh,
        in_specs=in_specs,
        out_specs=(wide, wide, tall, P()),
        check_vma=False,
    )
```

profile of v0, /device:TPU:0, one launch (start us, length us, event | category | flops | bytes accessed | tf_op | source)
XLA Modules:
  0.0 252.0 jit_solution(12324534410951306926)
XLA Ops:
  0.6 11.8 %shard_map.147 = bf16[4,32,1024]{2,1,0:T(8,128)(2,1)} custom-call(bf16[32,1024]{1,0:T(8,128)(2,1)} %x.3), custom_call_target="tpu_custom_call" | custom-call | tf_op jit(solution)/shard_map/pallas_call | solution.py:208
  12.5 25.2 %shard_map.148 = (bf16[4,128,4096]{2,1,0:T(8,128)(2,1)}, bf16[2,128,4096]{2,1,0:T(8,128)(2,1)}, f32[3,8,512]{2,1,0:T(8,128)}) custom-call(bf16[128,1024]{1,0:T(8,128)(2,1)} %bitcast.38, bf16[1024,4096]{1,0:T(8,128)(2,1)} %gate.1, bf16[1024,4096]{1,0:T(8,128)(2,1)} %up.1, bf16[1024,4096]{1,0:T(8,128)(2,1)} %refs_3_.2, bf16[1024,4096]{1,0:T(8,128)(2,1)} %refs_4_.1, ...), custom_call_target="tpu_custom_call" | custom-call | tf_op jit(solution)/shard_map/pallas_call | solution.py:393
  37.7 47.5 %shard_map.149 = (bf16[2,8,16,4096]{3,2,1,0:T(8,128)(2,1)}, f32[16,4096]{1,0:T(8,128)}, f32[16,4096]{1,0:T(8,128)}, f32[16,4096]{1,0:T(8,128)}, f32[16,4096]{1,0:T(8,128)}) custom-call(bf16[4,4,2,16,4096]{4,3,2,1,0:T(8,128)(2,1)} %bitcast.35), custom_call_target="tpu_custom_call" | custom-call | tf_op jit(solution)/shard_map/pallas_call | solution.py:167
  85.2 17.3 %shard_map.150 = (f32[256,1024]{1,0:T(8,128)}, f32[256,1024]{1,0:T(8,128)}, f32[256,1024]{1,0:T(8,128)}, f32[3,8,1024]{2,1,0:T(8,128)}) custom-call(bf16[256,4096]{1,0:T(8,128)(2,1)} %bitcast.37, bf16[4096,1024]{1,0:T(8,128)(2,1)} %down.3, bf16[4096,1024]{1,0:T(8,128)(2,1)} %refs_2_.1, bf16[4096,1024]{1,0:T(8,128)(2,1)} %refs_3_.3), custom_call_target="tpu_custom_call" | custom-call | tf_op jit(solution)/shard_map/pallas_call | solution.py:430
  102.5 2.9 %fusion.10 = (f32[128,1024]{1,0:T(8,128)}, f32[128,1024]{1,0:T(8,128)}, f32[128,1024]{1,0:T(8,128)S(1)}, bf16[128,1024]{1,0:T(8,128)(2,1)S(1)}, f32[128,1024]{1,0:T(8,128)}) fusion(f32[256,1024]{1,0:T(8,128)} %get-tuple-element.27, f32[256,1024]{1,0:T(8,128)} %get-tuple-element.21, f32[256,1024]{1,0:T(8,128)} %get-tuple-element.20), kind=kLoop, calls=%fused_computation.27 | loop fusion | flops 262144 | bytes 4980736 | tf_op jit(solution)/shard_map/slice | solution.py:540
  105.4 1.1 slice.70
  106.5 0.8 pad_maximum_fusion.3.x
  107.3 26.9 %shard_map.151 = bf16[2,4,32,1024]{3,2,1,0:T(8,128)(2,1)} custom-call(bf16[2,4,32,1024]{3,2,1,0:T(8,128)(2,1)} %pad_maximum_fusion.3.x, bf16[32,1024]{1,0:T(8,128)(2,1)} %targets.1), custom_call_target="tpu_custom_call" | custom-call | tf_op jit(solution)/shard_map/pallas_call | solution.py:267
  134.3 11.6 %shard_map.152 = bf16[2,128,4096]{2,1,0:T(8,128)(2,1)} custom-call(bf16[256,1024]{1,0:T(8,128)(2,1)} %bitcast.28, bf16[4096,1024]{1,0:T(8,128)(2,1)} %down.3, bf16[4096,1024]{1,0:T(8,128)(2,1)} %refs_2_.1), custom_call_target="tpu_custom_call" | custom-call | tf_op jit(solution)/shard_map/pallas_call | solution.py:462
  145.9 34.0 %shard_map.153 = bf16[2,8,16,4096]{3,2,1,0:T(8,128)(2,1)} custom-call(bf16[2,4,2,16,4096]{4,3,2,1,0:T(8,128)(2,1)} %bitcast.36, f32[16,4096]{1,0:T(8,128)} %get-tuple-element.22.refs_1_, f32[16,4096]{1,0:T(8,128)} %get-tuple-element.23.refs_2_, f32[16,4096]{1,0:T(8,128)} %get-tuple-element.24.refs_3_, f32[16,4096]{1,0:T(8,128)} %get-tuple-element.25.refs_4_), custom_call_target="tpu_custom_call" | custom-call | tf_op jit(solution)/shard_map/pallas_call | solution.py:167
  180.0 0.0 copy-start.6
  180.0 0.0 copy-start.5
  180.0 1.8 fusion.9
  181.8 0.0 copy-start.2
  181.8 0.0 copy-start.3
  181.8 0.4 fusion.13
  182.3 0.0 copy-done.6
  182.3 0.2 fusion.12
  182.5 1.0 fusion.6
  183.6 0.0 copy-done.5
  183.6 0.2 fusion.8
  183.8 0.0 copy-done.2
  183.8 0.0 copy-done.3
  183.8 0.0 copy-start.7
  183.8 0.0 copy-start.8
  183.8 1.0 copy-done.7
  184.8 0.7 fusion.7
  185.5 0.0 copy-done.8
  185.5 0.0 copy-done
  185.6 0.0 copy-start.1
  185.6 1.0 fusion.5
  187.8 0.0 copy-start.4
  187.8 1.4 pad_maximum_fusion.2
  189.3 1.3 pad_maximum_fusion.1
  190.5 0.0 copy-start.9
  190.5 0.0 copy-start.10
  190.5 1.2 fusion.3
  191.7 0.0 copy-done.1
  191.7 3.4 %fusion = (f32[]{:T(128)}, f32[]{:T(128)}) fusion(bf16[2,8,16,4096]{3,2,1,0:T(8,128)(2,1)S(1)} %copy-done.1, bf16[4,128,4096]{2,1,0:T(8,128)(2,1)S(1)} %copy-done.4, bf16[2,128,4096]{2,1,0:T(8,128)(2,1)} %get-tuple-element.26), kind=kLoop, calls=%fused_computation.2 | loop fusion | flops 7340030 | bytes 6291464 | tf_op jit(solution)/shard_map/reduce_sum | solution.py:543
  197.7 0.1 reduce_sum.79
  197.8 0.1 reduce_sum.78
  197.9 0.1 select_maximum_fusion
  198.0 0.7 broadcast_in_dim.2.x
  199.3 14.6 %shard_map.154.scales = f32[8,128]{1,0:T(8,128)} custom-call(f32[8,128]{1,0:T(8,128)} %broadcast_in_dim.2.x, f32[1]{0:T(128)S(6)} %copy.16.beta_prev), custom_call_target="tpu_custom_call" | custom-call | tf_op jit(solution)/shard_map/pallas_call | solution.py:332
  213.9 3.1 %pad_maximum_fusion.refs_0_ = bf16[256,4096]{1,0:T(8,128)(2,1)} fusion(bf16[128,4096]{1,0:T(8,128)(2,1)} %bitcast.46, bf16[128,4096]{1,0:T(8,128)(2,1)} %bitcast.44), kind=kLoop, calls=%fused_computation.4 | loop fusion | flops 4194304 | bytes 4194304 | tf_op jit(solution)/shard_map/concatenate | solution.py:534
  217.0 12.2 %shard_map.156 = bf16[4096,1024]{1,0:T(8,128)(2,1)} custom-call(f32[8,128]{1,0:T(8,128)} %shard_map.154.scales, bf16[256,4096]{1,0:T(8,128)(2,1)} %pad_maximum_fusion.refs_0_, bf16[256,1024]{1,0:T(8,128)(2,1)} %bitcast.29, bf16[4096,1024]{1,0:T(8,128)(2,1)} %refs_2_.1, bf16[4096,1024]{1,0:T(8,128)(2,1)} %refs_3_.3), custom_call_target="tpu_custom_call" | custom-call | tf_op jit(solution)/shard_map/pallas_call | solution.py:490
  229.2 21.5 %shard_map.155 = (bf16[1024,4096]{1,0:T(8,128)(2,1)}, bf16[1024,4096]{1,0:T(8,128)(2,1)}) custom-call(f32[8,128]{1,0:T(8,128)} %shard_map.154.scales, bf16[128,1024]{1,0:T(8,128)(2,1)} %bitcast.39, bf16[128,4096]{1,0:T(8,128)(2,1)} %bitcast.34, bf16[128,4096]{1,0:T(8,128)(2,1)} %bitcast.32, bf16[1024,4096]{1,0:T(8,128)(2,1)} %refs_3_.2, ...), custom_call_target="tpu_custom_call" | custom-call | tf_op jit(solution)/shard_map/pallas_call | solution.py:490
  250.7 1.3 slice_reduce_fusion
  (5 shorter events, 0.0 us)
Async XLA Ops:
  180.0 2.3 copy-start.6
  180.0 3.6 %copy-start.5 = (bf16[2,8,16,4096]{3,2,1,0:T(8,128)(2,1)S(1)}, bf16[2,8,16,4096]{3,2,1,0:T(8,128)(2,1)}, u32[]{:S(2)}) copy-start(bf16[2,8,16,4096]{3,2,1,0:T(8,128)(2,1)} %get-tuple-element.19) | copy-start | bytes 6291460
  181.8 2.0 copy-start.2
  181.8 2.0 copy-start.3
  183.6 2.0 copy-start
  183.8 1.0 copy-start.7
  183.8 1.7 copy-start.8
  185.6 6.2 %copy-start.1 = (bf16[2,8,16,4096]{3,2,1,0:T(8,128)(2,1)S(1)}, bf16[2,8,16,4096]{3,2,1,0:T(8,128)(2,1)}, u32[]{:S(2)}) copy-start(bf16[2,8,16,4096]{3,2,1,0:T(8,128)(2,1)} %shard_map.153) | copy-start | bytes 6291460
  187.8 3.9 %copy-start.4 = (bf16[4,128,4096]{2,1,0:T(8,128)(2,1)S(1)}, bf16[4,128,4096]{2,1,0:T(8,128)(2,1)}, u32[]{:S(2)}) copy-start(bf16[4,128,4096]{2,1,0:T(8,128)(2,1)} %get-tuple-element.18) | copy-start | bytes 12582916
  190.5 7.2 %copy-start.9 = (f32[3,8,1024]{2,1,0:T(8,128)S(1)}, f32[3,8,1024]{2,1,0:T(8,128)}, u32[]{:S(2)}) copy-start(f32[3,8,1024]{2,1,0:T(8,128)} %get-tuple-element.29) | copy-start | bytes 294916
  190.5 7.3 %copy-start.10 = (f32[3,8,512]{2,1,0:T(8,128)S(1)}, f32[3,8,512]{2,1,0:T(8,128)}, u32[]{:S(2)}) copy-start(f32[3,8,512]{2,1,0:T(8,128)} %get-tuple-element.28) | copy-start | bytes 147460
where the time goes:
time: 253 us; the launch traced here: 252 us
  Pallas kernels  223 us (88%)
  other arithmetic  14.4 us (6%)
  local copies, waits for them, and re-layouts  6.1 us (2%)
  between operations  5.35 us (2%)
  matrix products  3.4 us (1%)
    pallas_call x2, Pallas kernels, width_exchange(): pl.pallas_call(functools.partial(width_kernel, n, kinds, rows_of, keeps_i...  81.5 us
    pallas_call x2, Pallas kernels, next_parts(): pl.pallas_call(functools.partial(next_kernel, count), grid=(height // til...  33.7 us
    pallas_call x1, Pallas kernels, output_exchange(): pl.pallas_call(functools.partial(output_kernel, t), out_shape=jax.ShapeDt...  26.9 us
    pallas_call x1, Pallas kernels, front_products(): pl.pallas_call(front_kernel, grid=(width // tile,), out_shape=(jax.ShapeD...  25.2 us
    pallas_call x1, Pallas kernels, middle_products(): pl.pallas_call(middle_kernel, grid=(depth // tile,), out_shape=[jax.Shape...  17.3 us
    pallas_call x1, Pallas kernels, totals_exchange(): pl.pallas_call(functools.partial(totals_kernel, n, t, entries), out_shape...  14.6 us
    pallas_call x1, Pallas kernels, tokens_exchange(): pl.pallas_call(functools.partial(tokens_kernel, t), out_shape=jax.ShapeDt...  11.8 us
    pallas_call x1, Pallas kernels, back_products(): pl.pallas_call(back_kernel, grid=(width // tile,), out_shape=jax.ShapeDty...  11.6 us

commit v1 on v0

v1 whole, which is shorter than its diff:
```python
import functools

import jax
import jax.numpy as jnp
from jax import lax
from jax.experimental import pallas as pl
from jax.experimental.pallas import tpu as pltpu
from jax.sharding import PartitionSpec as P

MESH = pl.DeviceIdType.MESH
VMEM = pltpu.VMEM
DMA = pltpu.SemaphoreType.DMA
ANY = pl.BlockSpec(memory_space=pl.ANY)
WHOLE = pl.BlockSpec(memory_space=pltpu.VMEM)
F32 = jnp.float32
BF16 = jnp.bfloat16
LIMIT = 62 * 1024 * 1024


def tile_of(size, most):
    tile = min(size, most)
    while size % tile:
        tile //= 2
    return tile


def dot(one, two):
    return jnp.dot(one, two, preferred_element_type=F32)


def against(one, two):
    return lax.dot_general(one, two, (((1,), (1,)), ((), ())), preferred_element_type=F32)


def greet(targets):
    barrier = pltpu.get_barrier_semaphore()
    for target in targets:
        pl.semaphore_signal(barrier, inc=1, device_id=target, device_id_type=MESH)
    pl.semaphore_wait(barrier, len(targets))


def remote(src, dst, send_sem, recv_sem, target):
    return pltpu.make_async_remote_copy(
        src_ref=src, dst_ref=dst, send_sem=send_sem, recv_sem=recv_sem, device_id=target, device_id_type=MESH
    )


def folded(values, width=None):
    rows, cols = values.shape
    return values.reshape(rows // 8, 8, cols).sum(axis=0)


def lanes(values):
    total = values[:, :128]
    for at in range(128, values.shape[1], 128):
        total = total + values[:, at : at + 128]
    return total


class Width:
    def __init__(self, n, phases, chunks, kinds, share, width):
        self.n, self.phases, self.chunks, self.kinds = n, phases, chunks, kinds
        self.share, self.width = share, width
        self.steps = phases * chunks
        self.ys, self.xs = 2, n // 4
        self.step = width // chunks

    def scratch(self):
        p, y, x, share, width, v = self.phases, self.ys, self.xs, self.share, self.width, self.steps
        return [
            VMEM((p, 2, y, x, 2, share, width), BF16),
            VMEM((p, 2, y, x, share, width), BF16),
            VMEM((p, 2, y, x, share, width), BF16),
            VMEM((p, x, y, share, width), BF16),
            VMEM((p, x, share, width), BF16),
            VMEM((p, share, width), BF16),
            VMEM((p, x, share, width), BF16),
            VMEM((p, share, width), BF16),
            VMEM((p, x, share, width), BF16),
            VMEM((self.kinds, y, x, 2, share, width), BF16),
        ] + [
            DMA((v,)), DMA((v,)),
            DMA((v, x)), DMA((v, x)),
            DMA((v,)), DMA((v,)),
            DMA((v,)), DMA((v,)),
            DMA((v, x)), DMA((v, x)),
            DMA((v, x)), DMA((v, x)),
            DMA((v,)), DMA((v,)),
            DMA((v, x)), DMA((v, x)),
            DMA((v, x)), DMA((v, x)),
            DMA((v, y * x)), DMA((v, y * x)),
        ]

    def bind(self, refs):
        (self.x, self.mate_in, self.paired, self.x1, self.y1, self.y2, self.x2, self.sa, self.sb, self.full) = refs[:10]
        sems = refs[10:]
        self.sems = [(sems[i], sems[i + 1]) for i in range(0, len(sems), 2)]
        me = lax.axis_index("dp")
        self.core = lax.rem(me, 2)
        chip = lax.div(me, 2)
        self.px, self.py = lax.rem(chip, self.xs), lax.div(chip, self.xs)
        self.qy = 1 - self.py
        self.mate = self.at(self.py, self.px, 1 - self.core)
        self.across = self.at(self.qy, self.px, self.core)
        self.to = [lax.rem(self.px + s, self.xs) for s in range(self.xs)]
        self.off = [lax.rem(self.px + self.xs - s, self.xs) for s in range(self.xs)]

    def at(self, y, x, core):
        return {"dp": (y * self.xs + x) * 2 + core}

    def partners(self):
        row = [self.at(self.py, self.to[s], self.core) for s in range(1, self.xs)]
        return [self.mate, self.across] + row

    def cols(self, v, part=0, parts=1):
        size = self.step // parts
        start = lax.rem(v, self.chunks) * self.step + part * size
        return pl.ds(pl.multiple_of(start, size), size)

    def phase(self, v):
        return lax.div(v, self.chunks)

    def row(self, s):
        return self.at(self.py, self.to[s], self.core)

    def mated(self, v):
        p, cols, (s, r) = self.phase(v), self.cols(v), self.sems[0]
        return remote(
            self.x.at[p, :, :, :, 1 - self.core, :, cols], self.mate_in.at[p, :, :, :, :, cols], s.at[v], r.at[v], self.mate
        )

    def first_x(self, v, k):
        p, cols, (s, r) = self.phase(v), self.cols(v), self.sems[1]
        return remote(
            self.paired.at[p, 0, :, self.to[k], :, cols], self.x1.at[p, self.px, :, :, cols], s.at[v, k], r.at[v, k], self.row(k)
        )

    def first_y(self, v):
        p, cols, (s, r) = self.phase(v), self.cols(v), self.sems[2]
        return remote(
            self.paired.at[p, 1, self.qy, :, :, cols], self.y1.at[p, :, :, cols], s.at[v], r.at[v], self.across
        )

    def second_y(self, v):
        p, cols, (s, r) = self.phase(v), self.cols(v), self.sems[3]
        return remote(self.sa.at[p, :, cols], self.y2.at[p, :, cols], s.at[v], r.at[v], self.across)

    def second_x(self, v, k):
        p, cols, (s, r) = self.phase(v), self.cols(v), self.sems[4]
        return remote(
            self.sb.at[p, self.to[k], :, cols], self.x2.at[p, self.px, :, cols], s.at[v, k], r.at[v, k], self.row(k)
        )

    def block(self, v, y, x):
        if self.phases > 1:
            return self.full.at[self.phase(v), y, x, self.core, :, self.cols(v)]
        return self.full.at[:, y, x, self.core, :, self.cols(v)]

    def half(self, v, y, x, part):
        if self.phases > 1:
            parts = 2 if self.step % 256 == 0 else 1
            if parts == 1:
                rows = pl.ds(part * (self.share // 2), self.share // 2)
                return self.full.at[self.phase(v), y, x, self.core, rows, self.cols(v)]
            return self.full.at[self.phase(v), y, x, self.core, :, self.cols(v, part, 2)]
        return self.full.at[part, y, x, self.core, :, self.cols(v)]

    def gather_x(self, v, k):
        s, r = self.sems[5]
        mine = self.block(v, self.py, self.px)
        return remote(mine, mine, s.at[v, k], r.at[v, k], self.row(k))

    def gather_y(self, v):
        s, r = self.sems[6]
        mine = self.block(v, self.py, self.px)
        return remote(mine, mine, s.at[v], r.at[v], self.across)

    def pass_y(self, v, k):
        s, r = self.sems[7]
        piece = self.half(v, self.py, self.off[k], 0)
        return remote(piece, piece, s.at[v, k], r.at[v, k], self.across)

    def pass_x(self, v, k):
        s, r = self.sems[8]
        piece = self.half(v, self.qy, self.px, 1)
        return remote(piece, piece, s.at[v, k], r.at[v, k], self.row(k))

    def hand(self, v, role):
        s, r = self.sems[9]
        y, k = (self.py, role) if role < self.xs else (self.qy, role - self.xs)
        piece = self.block(v, y, self.off[k])
        return remote(piece, piece, s.at[v, role], r.at[v, role], self.mate)

    def put(self, v, kind, rows):
        p, cols = self.phase(v), self.cols(v)
        shape = (self.ys, self.xs, 2, self.share, self.step)
        self.x[p, kind, :, :, :, :, cols] = rows.astype(BF16).reshape(shape)

    def pair(self, v):
        p, cols = self.phase(v), self.cols(v)
        self.mated(v).wait_recv()
        self.paired[p, :, :, :, :, cols] = (
            self.x[p, :, :, :, self.core, :, cols].astype(F32) + self.mate_in[p, :, :, :, :, cols].astype(F32)
        ).astype(BF16)
        for k in range(1, self.xs):
            self.first_x(v, k).start()
        self.first_y(v).start()

    def cross(self, v):
        p, cols = self.phase(v), self.cols(v)
        for k in range(1, self.xs):
            self.first_x(v, k).wait_recv()
        total = self.paired[p, 0, self.qy, self.px, :, cols].astype(F32)
        for k in range(1, self.xs):
            total = total + self.x1[p, self.off[k], self.qy, :, cols].astype(F32)
        self.sa[p, :, cols] = total.astype(BF16)
        self.second_y(v).start()
        self.first_y(v).wait_recv()
        for k in range(1, self.xs):
            total = self.paired[p, 1, self.py, self.to[k], :, cols].astype(F32) + self.y1[
                p, self.to[k], :, cols
            ].astype(F32)
            self.sb[p, self.to[k], :, cols] = total.astype(BF16)
            self.second_x(v, k).start()

    def totals(self, v):
        p, cols = self.phase(v), self.cols(v)
        self.second_y(v).wait_recv()
        for k in range(1, self.xs):
            self.second_x(v, k).wait_recv()
        one = self.paired[p, 0, self.py, self.px, :, cols].astype(F32) + self.y2[p, :, cols].astype(F32)
        two = self.paired[p, 1, self.py, self.px, :, cols].astype(F32) + self.y1[p, self.px, :, cols].astype(F32)
        for k in range(1, self.xs):
            one = one + self.x1[p, self.off[k], self.py, :, cols].astype(F32)
            two = two + self.x2[p, self.off[k], :, cols].astype(F32)
        return one, two

    def keep(self, v, kind, rows):
        self.full[kind, self.py, self.px, self.core, :, self.cols(v)] = rows.astype(BF16)

    def spread(self, v):
        for k in range(1, self.xs):
            self.gather_x(v, k).start()
        self.gather_y(v).start()
        self.hand(v, 0).start()

    def relay(self, v):
        for k in range(1, self.xs):
            self.gather_x(v, k).wait_recv()
            self.pass_y(v, k).start()
        self.gather_y(v).wait_recv()
        for k in range(1, self.xs):
            self.pass_x(v, k).start()
        for role in range(1, self.xs + 1):
            self.hand(v, role).start()

    def relay_last(self, v):
        for k in range(1, self.xs):
            self.pass_y(v, k).wait_recv()
            self.pass_x(v, k).wait_recv()
            self.hand(v, self.xs + k).start()

    def complete(self, v):
        for role in range(2 * self.xs):
            self.hand(v, role).wait_recv()

    def rows(self, v, kind):
        cols = self.cols(v)
        return self.full[kind, :, :, :, :, cols].reshape(self.n * self.share, self.step)

    def drain(self):
        @pl.loop(0, self.steps)
        def _(v):
            self.mated(v).wait_send()
            self.first_y(v).wait_send()
            self.second_y(v).wait_send()
            self.gather_y(v).wait_send()
            for k in range(1, self.xs):
                for copy in (self.first_x, self.second_x, self.gather_x, self.pass_y, self.pass_x):
                    copy(v, k).wait_send()
            for role in range(2 * self.xs):
                self.hand(v, role).wait_send()


LAGS = dict(pair=1, cross=3, totals=5, relay=7, last=9, done=10)


def staged(i, lag, steps, body):
    v = i - lag

    @pl.when((v >= 0) & (v < steps))
    def _():
        body(v)


DEEP = 4
SLOTS = 3


def squares(along_ref, before_ref, norms):
    rows, width = along_ref.shape
    step = tile_of(rows, 32)

    def body(i, sums):
        at = pl.ds(pl.multiple_of(i * step, step), step)
        along = along_ref[at, :].astype(F32)
        before = before_ref[at, :].astype(F32)
        products = (along * along, along * before, before * before)
        return tuple(have + folded(product) for have, product in zip(sums, products))

    zero = jnp.zeros((8, width), F32)
    sums = lax.fori_loop(0, rows // step, body, (zero, zero, zero))
    for kind in range(3):
        norms[kind] += lanes(sums[kind])


def early_kernel(n, t, width, *refs):
    (tokens, targets, gate, up, down, along_gate, along_up, along_down, before_gate, before_up, before_down) = refs[:11]
    (out_tokens, out_units, out_keeps, out_grads, out_before, norms) = refs[11:17]
    (tok, keeps, bx, weights, downs, alongs, wide, tall, acc, zx, zin, gz) = refs[17:29]
    (tok_s, tok_r, w_sem, d_sem, wide_sem, tall_sem, zs, zr, gs, gr, o_sem) = refs[29:40]
    width.bind(refs[40:])
    chunks, steps, step = width.chunks, width.steps, width.step
    share, depth = tokens.shape
    rows = t * share
    me = lax.axis_index("tp")
    spots = [lax.rem(me + s, t) for s in range(1, t)]
    sources = [lax.rem(me + t - s, t) for s in range(1, t)]

    def col(v):
        return width.cols(v)

    def load(v, one, two, start):
        slot = lax.rem(v, DEEP)
        for kind, ref in enumerate((one, two)):
            copy = pltpu.make_async_copy(ref.at[:, col(v)], weights.at[slot, kind], w_sem.at[slot, kind])
            if start:
                copy.start()
            else:
                copy.wait()

    def fetch(v):
        @pl.when(v < chunks)
        def _():
            load(v, gate, up, True)

        @pl.when((v >= chunks) & (v < steps))
        def _():
            load(v, along_gate, along_up, True)

    for v in range(DEEP):
        fetch(jnp.int32(v))

    def wide_copies(one, two, c):
        slot = lax.rem(c, SLOTS)
        return [
            pltpu.make_async_copy(ref.at[:, col(c)], wide.at[slot, kind], wide_sem.at[slot, kind])
            for kind, ref in enumerate((one, two))
            if ref is not None
        ]

    def tall_copies(c):
        slot = lax.rem(c, SLOTS)
        return [
            pltpu.make_async_copy(ref.at[col(c), :], tall.at[slot, kind], tall_sem.at[slot, kind])
            for kind, ref in enumerate((along_down, before_down))
        ]

    def open_stream(copies):
        for c in range(min(SLOTS, chunks)):
            for copy in copies(jnp.int32(c)):
                copy.start()

    def run_stream(copies, body):
        @pl.loop(0, chunks)
        def _(c):
            for copy in copies(c):
                copy.wait()
            body(c, lax.rem(c, SLOTS))

            @pl.when(c + SLOTS < chunks)
            def _():
                for copy in copies(c + SLOTS):
                    copy.start()

    gate_stream = functools.partial(wide_copies, along_gate, before_gate)
    up_stream = functools.partial(wide_copies, along_up, before_up)
    again_stream = functools.partial(wide_copies, None, before_gate)
    open_stream(gate_stream)
    load_down = pltpu.make_async_copy(down, downs, d_sem.at[0])
    load_along = pltpu.make_async_copy(along_down, alongs, d_sem.at[1])

    norms[...] = jnp.zeros_like(norms)
    greet(width.partners() + [{"tp": spot} for spot in spots])

    def gather(i):
        return remote(tokens, tok.at[me], tok_s.at[i], tok_r.at[i], {"tp": spots[i]})

    for i in range(t - 1):
        gather(i).start()
    tok[me] = tokens[...]

    def norm_wide(c, slot):
        squares(wide.at[slot, 0], wide.at[slot, 1], norms)

    run_stream(gate_stream, norm_wide)
    load_down.start()
    load_along.start()
    for i in range(t - 1):
        gather(i).wait_recv()

    def everyone():
        return tok[...].reshape(rows, depth)

    acc[...] = jnp.zeros_like(acc)

    def front(v):
        load(v, gate, up, False)
        slot = lax.rem(v, DEEP)
        for kind in range(2):
            width.put(v, kind, dot(everyone(), weights[slot, kind]))
        width.mated(v).start()
        fetch(v + DEEP)

    def sums(v):
        one, two = width.totals(v)
        cols = col(v)
        p = width.phase(v)

        @pl.when(p == 0)
        def _():
            keeps[0, :, cols] = one
            keeps[1, :, cols] = two
            width.keep(v, 0, one * jax.nn.sigmoid(one) * two)

        @pl.when(p == 1)
        def _():
            keeps[2, :, cols] = one
            keeps[3, :, cols] = two
            gate_sum, up_sum = keeps[0, :, cols], keeps[1, :, cols]
            logistic = jax.nn.sigmoid(gate_sum)
            slope = logistic * (1.0 + gate_sum * (1.0 - logistic))
            width.keep(v, 1, slope * up_sum * one + gate_sum * logistic * two)

        width.spread(v)

    def middle(v):
        width.complete(v)
        p, at = width.phase(v), col(v)

        @pl.when(v == 0)
        def _():
            load_down.wait()

        @pl.when(v == chunks)
        def _():
            load_along.wait()

        @pl.when(p == 0)
        def _():
            acc[0] += dot(width.rows(v, 0), downs[at, :])

        @pl.when(p == 1)
        def _():
            acc[1] += dot(width.rows(v, 1), downs[at, :]) + dot(width.rows(v, 0), alongs[at, :])

    def z_first(p, i):
        return remote(zx.at[p, spots[i]], zin.at[p, me], zs.at[p, i], zr.at[p, i], {"tp": spots[i]})

    def z_second(p, i):
        return remote(gz.at[p, me], gz.at[p, me], gs.at[p, i], gr.at[p, i], {"tp": spots[i]})

    def z_send(p):
        zx[p] = acc[p].astype(BF16).reshape(t, share, depth)
        for i in range(t - 1):
            z_first(p, i).start()

    def z_finish(p):
        for i in range(t - 1):
            z_first(p, i).wait_recv()
        total = zx[p, me].astype(F32)
        for at in sources:
            total = total + zin[p, at].astype(F32)
        if p == 0:
            total = total - targets[...].astype(F32)
        gz[p, me] = (total / rows).astype(BF16)
        for i in range(t - 1):
            z_second(p, i).start()

    ready = chunks - 1 + LAGS["done"]
    last = steps + LAGS["done"]
    settle = min(ready + 6, last - 1)

    @pl.loop(0, last)
    def _(i):
        staged(i, 0, steps, front)
        staged(i, LAGS["cross"], steps, width.cross)
        staged(i, LAGS["totals"], steps, sums)
        staged(i, LAGS["relay"], steps, width.relay)
        staged(i, LAGS["last"], steps, width.relay_last)
        staged(i, LAGS["done"], steps, middle)
        staged(i, LAGS["pair"], steps, width.pair)

        @pl.when(i == ready)
        def _():
            z_send(0)

        @pl.when(i == settle)
        def _():
            z_finish(0)

    z_send(1)
    open_stream(up_stream)

    def before_of(kind):
        def body(c, slot):
            bx[kind, :, col(c)] = dot(everyone(), wide[slot, 1]).astype(BF16)

        return body

    def norm_and_before(c, slot):
        norm_wide(c, slot)
        before_of(1)(c, slot)

    stores = [
        pltpu.make_async_copy(tok, out_tokens, o_sem.at[0]),
        pltpu.make_async_copy(width.full, out_units, o_sem.at[1]),
        pltpu.make_async_copy(keeps, out_keeps, o_sem.at[2]),
    ]
    for store in stores:
        store.start()
    run_stream(up_stream, norm_and_before)
    open_stream(tall_copies)
    open_stream(again_stream)
    z_finish(1)

    def norm_tall(c, slot):
        squares(tall.at[slot, 0], tall.at[slot, 1], norms)

    run_stream(tall_copies, norm_tall)
    run_stream(again_stream, before_of(0))
    stores.append(pltpu.make_async_copy(bx, out_before, o_sem.at[3]))
    stores[-1].start()
    for p in range(2):
        for i in range(t - 1):
            z_second(p, i).wait_recv()
    stores.append(pltpu.make_async_copy(gz, out_grads, o_sem.at[4]))
    stores[-1].start()
    for i in range(t - 1):
        gather(i).wait_send()
        for p in range(2):
            z_first(p, i).wait_send()
            z_second(p, i).wait_send()
    width.drain()
    for store in stores:
        store.wait()


def early(n, t, tokens, targets, gate, up, down, along_gate, along_up, along_down, before_gate, before_up, before_down):
    share, depth = tokens.shape
    width = gate.shape[1]
    rows = t * share
    chunks = width // tile_of(width, max(128, width // 8))
    plan = Width(n, 2, chunks, 2, rows // n, width)
    step = plan.step
    keeps = (4, plan.share, width)
    units = (2, plan.ys, plan.xs, 2, plan.share, width)
    z = (2, t, share, depth)
    return pl.pallas_call(
        functools.partial(early_kernel, n, t, plan),
        out_shape=[
            jax.ShapeDtypeStruct((t, share, depth), BF16),
            jax.ShapeDtypeStruct(units, BF16),
            jax.ShapeDtypeStruct(keeps, F32),
            jax.ShapeDtypeStruct(z, BF16),
            jax.ShapeDtypeStruct((2, rows, width), BF16),
            jax.ShapeDtypeStruct((3, 8, 128), F32),
        ],
        in_specs=[WHOLE, WHOLE] + [ANY] * 9,
        out_specs=[ANY] * 5 + [WHOLE],
        scratch_shapes=[
            VMEM((t, share, depth), BF16),
            VMEM(keeps, F32),
            VMEM((2, rows, width), BF16),
            VMEM((DEEP, 2, depth, step), BF16),
            VMEM((width, depth), BF16),
            VMEM((width, depth), BF16),
            VMEM((SLOTS, 2, depth, step), BF16),
            VMEM((SLOTS, 2, step, depth), BF16),
            VMEM((2, rows, depth), F32),
            VMEM(z, BF16),
            VMEM(z, BF16),
            VMEM(z, BF16),
            DMA((t - 1,)),
            DMA((t - 1,)),
            DMA((DEEP, 2)),
            DMA((2,)),
            DMA((SLOTS, 2)),
            DMA((SLOTS, 2)),
            DMA((2, t - 1)),
            DMA((2, t - 1)),
            DMA((2, t - 1)),
            DMA((2, t - 1)),
            DMA((5,)),
        ]
        + plan.scratch(),
        compiler_params=pltpu.CompilerParams(collective_id=1, has_side_effects=True, vmem_limit_bytes=LIMIT),
    )(tokens, targets, gate, up, down, along_gate, along_up, along_down, before_gate, before_up, before_down)


def late_kernel(n, t, entries, width, *refs):
    (tokens, units, keeps_in, grads_in, before_in, norms, down, along, before, beta_prev) = refs[:10]
    (out_dirs, scales) = refs[10:12]
    (grads, hidden, keeps, bx, downs, alongs, befores, sums, gram, swap_gram) = refs[12:22]
    (dp_in, total_dp, tp_in) = refs[22:25]
    (in_sem, m_sem, o_sem, s1, r1, s2, r2) = refs[25:32]
    width.bind(refs[32:])
    chunks, steps, step = width.chunks, width.steps, width.step
    depth = down.shape[1]
    rows = n * width.share
    dp, tp = lax.axis_index("dp"), lax.axis_index("tp")
    dp_spots = [lax.rem(dp + s, n) for s in range(1, n)]
    tp_spots = [lax.rem(tp + s, t) for s in range(1, t)]

    loads = [
        pltpu.make_async_copy(src, dst, in_sem.at[i])
        for i, (src, dst) in enumerate(((grads_in, grads), (units, hidden), (keeps_in, keeps), (before_in, bx)))
    ]

    def matrix(which, c):
        src, dst = ((down, downs), (along, alongs), (before, befores))[which]
        at = width.cols(c)
        return pltpu.make_async_copy(src.at[at, :], dst.at[at, :], m_sem.at[which, c])

    loads[0].start()
    for c in range(chunks):
        matrix(0, jnp.int32(c)).start()
        matrix(1, jnp.int32(c)).start()
        if c == 0:
            for load in loads[1:]:
                load.start()
    for c in range(chunks):
        matrix(2, jnp.int32(c)).start()
    sums[...] = jnp.zeros_like(sums)
    gram[...] = jnp.zeros_like(gram)
    swap_gram[...] = jnp.zeros_like(swap_gram)
    greet([{"dp": spot} for spot in dp_spots] + [{"tp": spot} for spot in tp_spots])
    for load in loads:
        load.wait()

    def both():
        return grads[...].reshape(2 * rows, depth)

    def unit(v, kind):
        return hidden[kind, :, :, :, :, width.cols(v)].reshape(rows, step)

    def crossed(which, v, products):
        value = products[:rows] * unit(v, 1).astype(F32) + products[rows:] * unit(v, 0).astype(F32)
        sums[which] += lanes(folded(value))

    def back(v):
        matrix(0, v).wait()
        matrix(1, v).wait()
        at = width.cols(v)
        weighted = against(both(), downs[at, :])
        moved = against(both(), alongs[at, :])
        width.put(v, 0, weighted[:rows])
        width.put(v, 1, weighted[rows:] + moved[:rows])
        width.mated(v).start()
        crossed(1, v, moved)

    def extra(v):
        matrix(2, v).wait()
        crossed(2, v, against(both(), befores[width.cols(v), :]))
        swapped = jnp.concatenate([unit(v, 1), unit(v, 0)])
        swap_gram[...] += against(swapped, swapped)

    def middle(v):
        grad_hidden, grad_hidden_dir = width.totals(v)
        cols = width.cols(v)
        gate_sum, up_sum, gate_dir, up_dir = (keeps[k, :, cols] for k in range(4))
        logistic = jax.nn.sigmoid(gate_sum)
        activation = gate_sum * logistic
        slope = logistic * (1.0 + gate_sum * (1.0 - logistic))
        curve = logistic * (1.0 - logistic) * (2.0 + gate_sum * (1.0 - 2.0 * logistic))
        grad_gate = (
            grad_hidden_dir * up_sum * slope + grad_hidden * up_dir * slope + grad_hidden * up_sum * curve * gate_dir
        ).astype(BF16)
        grad_up = (grad_hidden_dir * activation + grad_hidden * slope * gate_dir).astype(BF16)
        width.keep(v, 0, grad_gate)
        width.keep(v, 1, grad_up)
        width.spread(v)
        sums[1] += lanes(folded(grad_gate.astype(F32) * gate_dir + grad_up.astype(F32) * up_dir))

    def finish(v):
        width.complete(v)
        cols = width.cols(v)
        for kind in range(2):
            part = width.rows(v, kind)
            gram[...] += against(part, part)
            sums[2] += lanes(folded(part.astype(F32) * bx[kind, :, cols].astype(F32)))

    @pl.loop(0, steps + LAGS["done"])
    def _(i):
        staged(i, 0, steps, back)
        staged(i, LAGS["cross"], steps, width.cross)
        staged(i, LAGS["totals"], steps, middle)
        staged(i, LAGS["relay"], steps, width.relay)
        staged(i, LAGS["last"], steps, width.relay_last)
        staged(i, LAGS["done"], steps, finish)
        staged(i, LAGS["pair"], steps, width.pair)
        staged(i, LAGS["totals"], steps, extra)

    store = pltpu.make_async_copy(width.full, out_dirs, o_sem.at[0])
    store.start()
    every = tokens[...].reshape(rows, depth)
    sums[0] += lanes(folded(against(every, every) * gram[...])) + lanes(
        folded(against(both(), both()) * swap_gram[...])
    )
    shape = (1, 128)
    own = [jnp.full(shape, jnp.sum(sums[k])) for k in range(3)] + [jnp.full(shape, jnp.sum(norms[k])) for k in range(3)]
    for k in range(6):
        total_dp[k : k + 1] = own[k]
    total_dp[6:8] = jnp.zeros((2, 128), F32)
    dp_in[dp] = total_dp[...]

    first = [
        remote(total_dp, dp_in.at[dp], s1.at[i], r1.at[i], {"dp": spot}) for i, spot in enumerate(dp_spots)
    ]
    for copy in first:
        copy.start()
    for copy in first:
        copy.wait_recv()
    total = dp_in[0]
    for at in range(1, n):
        total = total + dp_in[at]
    tp_in[tp] = total
    second = [
        remote(tp_in.at[tp], tp_in.at[tp], s2.at[i], r2.at[i], {"tp": spot}) for i, spot in enumerate(tp_spots)
    ]
    for copy in second:
        copy.start()
    for copy in second:
        copy.wait_recv()
    total = tp_in[0]
    for at in range(1, t):
        total = total + tp_in[at]
    image_image, image_along, image_before = total[0:1], total[1:2], total[2:3]
    along_along, along_before, before_before = total[3:4], total[4:5], total[5:6]
    beta_old = beta_prev[0]
    alpha_coef = image_along / entries
    square = (
        image_image
        - 2.0 * alpha_coef * image_along
        - 2.0 * beta_old * image_before
        + alpha_coef * alpha_coef * along_along
        + 2.0 * alpha_coef * beta_old * along_before
        + beta_old * beta_old * before_before
    )
    beta_coef = jnp.sqrt(square / entries + 1e-06)
    inverse = 1.0 / beta_coef
    scales[0:1] = alpha_coef
    scales[1:2] = beta_coef
    scales[2:3] = inverse
    scales[3:4] = alpha_coef * inverse
    scales[4:5] = beta_old * inverse
    scales[5:8] = jnp.zeros((3, 128), F32)
    for copy in first + second:
        copy.wait_send()
    width.drain()
    store.wait()


def late(n, t, entries, tokens, units, keeps, grads, bx, norms, down, along, before, beta_prev):
    width, depth = down.shape
    rows = bx.shape[1]
    chunks = width // tile_of(width, max(128, width // 8))
    plan = Width(n, 1, chunks, 2, rows // n, width)
    small = (8, 128)
    return pl.pallas_call(
        functools.partial(late_kernel, n, t, entries, plan),
        out_shape=[jax.ShapeDtypeStruct(units.shape, BF16), jax.ShapeDtypeStruct(small, F32)],
        in_specs=[WHOLE] + [ANY] * 4 + [WHOLE] + [ANY] * 3 + [pl.BlockSpec(memory_space=pltpu.SMEM)],
        out_specs=[ANY, WHOLE],
        scratch_shapes=[
            VMEM(grads.shape, BF16),
            VMEM(units.shape, BF16),
            VMEM(keeps.shape, F32),
            VMEM(bx.shape, BF16),
            VMEM((width, depth), BF16),
            VMEM((width, depth), BF16),
            VMEM((width, depth), BF16),
            VMEM((3,) + small, F32),
            VMEM((rows, rows), F32),
            VMEM((2 * rows, 2 * rows), F32),
            VMEM((n,) + small, F32),
            VMEM(small, F32),
            VMEM((t,) + small, F32),
            DMA((4,)),
            DMA((3, chunks)),
            DMA((1,)),
            DMA((n - 1,)),
            DMA((n - 1,)),
            DMA((t - 1,)),
            DMA((t - 1,)),
        ]
        + plan.scratch(),
        compiler_params=pltpu.CompilerParams(collective_id=2, has_side_effects=True, vmem_limit_bytes=LIMIT),
    )(tokens, units, keeps, grads, bx, norms, down, along, before, beta_prev)


def transposed(one, two):
    return lax.dot_general(one, two, (((0,), (0,)), ((), ())), preferred_element_type=F32)


def next_kernel(scales, tokens, dirs, units, grads, along_gate, along_up, along_down, before_gate, before_up, before_down, out_gate, out_up, out_down, tall):
    inverse, alpha, beta = scales[2, 0], scales[3, 0], scales[4, 0]

    @pl.when(pl.program_id(0) == 0)
    def _():
        tall[...] = tokens[...].T

    def blend(image, along, before, out):
        out[...] = (image * inverse - along[...].astype(F32) * alpha - before[...].astype(F32) * beta).astype(BF16)

    blend(dot(tall[...], dirs[0]), along_gate, before_gate, out_gate)
    blend(dot(tall[...], dirs[1]), along_up, before_up, out_up)
    image = transposed(units[1], grads[0]) + transposed(units[0], grads[1])
    blend(image, along_down, before_down, out_down)


def next_parts(scales, tokens, dirs, units, grads, alongs, befores):
    rows, depth = tokens.shape
    width = dirs.shape[2]
    tile = tile_of(width, 256)
    wide = pl.BlockSpec((depth, tile), lambda i: (0, i))
    tall = pl.BlockSpec((tile, depth), lambda i: (i, 0))
    return pl.pallas_call(
        next_kernel,
        grid=(width // tile,),
        out_shape=[jax.ShapeDtypeStruct((depth, width), BF16)] * 2 + [jax.ShapeDtypeStruct((width, depth), BF16)],
        in_specs=[
            pl.BlockSpec(memory_space=pltpu.SMEM),
            pl.BlockSpec((rows, depth), lambda i: (0, 0)),
            pl.BlockSpec((2, rows, tile), lambda i: (0, 0, i)),
            pl.BlockSpec((2, rows, tile), lambda i: (0, 0, i)),
            pl.BlockSpec((2, rows, depth), lambda i: (0, 0, 0)),
        ]
        + [wide, wide, tall] * 2,
        out_specs=[wide, wide, tall],
        scratch_shapes=[VMEM((depth, rows), BF16)],
        compiler_params=pltpu.CompilerParams(vmem_limit_bytes=LIMIT),
    )(scales, tokens, dirs, units, grads, *alongs, *befores)


def on_device(
    n,
    t,
    tokens,
    targets,
    gate_weight,
    up_weight,
    down_weight,
    direction_gate,
    direction_up,
    direction_down,
    previous_gate,
    previous_up,
    previous_down,
    beta_prev,
):
    everyone, units, keeps, grads, bx, norms = early(
        n,
        t,
        tokens,
        targets,
        gate_weight,
        up_weight,
        down_weight,
        direction_gate,
        direction_up,
        direction_down,
        previous_gate,
        previous_up,
        previous_down,
    )
    entries = float(n * t * (gate_weight.size + up_weight.size + down_weight.size))
    dirs, scales = late(
        n, t, entries, everyone, units, keeps, grads, bx, norms, down_weight, direction_down, previous_down, beta_prev
    )
    rows, depth = bx.shape[1], tokens.shape[1]
    next_gate, next_up, next_down = next_parts(
        scales,
        everyone.reshape(rows, depth),
        dirs.reshape(bx.shape),
        units.reshape(bx.shape),
        grads.reshape(2, rows, depth),
        (direction_gate, direction_up, direction_down),
        (previous_gate, previous_up, previous_down),
    )
    return (next_gate, next_up, next_down, scales[:2, 0])


def solution(mesh):
    wide, tall = P("dp", "tp"), P("tp", "dp")
    in_specs = (tall, tall, wide, wide, tall, wide, wide, tall, wide, wide, tall, P())
    return jax.shard_map(
        functools.partial(on_device, mesh.shape["dp"], mesh.shape["tp"]),
        mesh=mesh,
        in_specs=in_specs,
        out_specs=(wide, wide, tall, P()),
        check_vma=False,
    )
```

time: 253 us -> 170 us (0.67)
  Pallas kernels: 223 us -> 167 us
  other arithmetic: 14.4 us -> 0 us
  local copies, waits for them, and re-layouts: 6.1 us -> 1.31 us
  between operations: 5.35 us -> 1.3 us
  matrix products: 3.4 us -> 0 us
    pallas_call x10 -> x3, Pallas kernels: 223 us -> 167 us  [the longest x1 83.6 us: early(): pl.pallas_call(functools.partial(early_kernel, n, t, plan), out_shape=[ja...]
    concatenate x4 -> x0, other arithmetic: 5.85 us -> none  [the longest x1 3.08 us: on_device(): swapped = jnp.concatenate([units[rows:], units[:rows]])]
    reduce_sum x4 -> x0, other arithmetic: 4.81 us -> none  [the longest x1 3.41 us: on_device(): jnp.sum(wide * x[2:].astype(F32)) + jnp.sum(tall * swapped_moved)]
    dot_general x5 -> x0, matrix products: 3.4 us -> none  [against(): lax.dot_general(one, two, (((1,), (1,)), ((), ())), preferred_element_typ...]
    slice x3 -> x0, local copies, waits for them, and re-layouts: 3.11 us -> none  [the longest x1 1.83 us: on_device(): gram = against(dirs[0], dirs[0]) + against(dirs[1], dirs[1])]
    slice x1 -> x0, other arithmetic: 2.91 us -> none  [on_device(): swapped_was = jnp.concatenate([was[rows:], was[:rows]])]
where the time goes in v1:
time: 170 us
  Pallas kernels  167 us (98%)
    pallas_call x1, Pallas kernels, early(): pl.pallas_call(functools.partial(early_kernel, n, t, plan), out_shape=[ja...  83.6 us
    pallas_call x1, Pallas kernels, late(): pl.pallas_call(functools.partial(late_kernel, n, t, entries, plan), out_s...  51.4 us
    pallas_call x1, Pallas kernels, next_parts(): pl.pallas_call(next_kernel, grid=(width // tile,), out_shape=[jax.ShapeDt...  32 us

profile of v1, /device:TPU:0, one launch (start us, length us, event | category | flops | bytes accessed | tf_op | source)
XLA Modules:
  0.0 169.6 jit_solution(4482995661986163628)
XLA Ops:
  0.6 83.6 %shard_map.147 = (bf16[4,32,1024]{2,1,0:T(8,128)(2,1)}, bf16[2,2,2,2,16,4096]{5,4,3,2,1,0:T(8,128)(2,1)}, f32[4,16,4096]{2,1,0:T(8,128)}, bf16[2,4,32,1024]{3,2,...) custom-call(bf16[32,1024]{1,0:T(8,128)(2,1)} %refs_0_.1, bf16[32,1024]{1,0:T(8,128)(2,1)} %refs_1_.1, ...), custom_call_target="tpu_custom_call" | custom-call | tf_op jit(solution)/shard_map/pallas_call | solution.py:569
  84.8 51.4 %shard_map.148 = (bf16[2,2,2,2,16,4096]{5,4,3,2,1,0:T(8,128)(2,1)}, f32[8,128]{1,0:T(8,128)}) custom-call(bf16[4,32,1024]{2,1,0:T(8,128)(2,1)} %get-tuple-element.15.refs_0_, bf16[2,2,2,2,16,4096]{5,4,3,2,1,0:T(8,128)(2,1)} %get-tuple-element.16.refs_1_, f32[4,16,4096]{2,1,0:T(8,128)} %get-tuple-element.17.refs_2_, ...), custom_call_target="tpu_custom_call" | custom-call | tf_op jit(solution)/shard_map/pallas_call | solution.py:780
  136.2 32.0 %shard_map.149 = (bf16[1024,4096]{1,0:T(8,128)(2,1)}, bf16[1024,4096]{1,0:T(8,128)(2,1)}, bf16[4096,1024]{1,0:T(8,128)(2,1)}) custom-call(f32[8,128]{1,0:T(8,128)} %get-tuple-element.21.scales, bf16[128,1024]{1,0:T(8,128)(2,1)} %bitcast.7, bf16[2,128,4096]{2,1,0:T(8,128)(2,1)} %bitcast.6, bf16[2,128,4096]{2,1,0:T(8,128)(2,1)} %bitcast.4, ...), custom_call_target="tpu_custom_call" | custom-call | tf_op jit(solution)/shard_map/pallas_call | solution.py:838
  168.3 1.3 slice_reduce_fusion

commit v2 on v1

--- a/solution.py
+++ b/solution.py
@@ -15,6 +15,8 @@
 F32 = jnp.float32
 BF16 = jnp.bfloat16
 LIMIT = 62 * 1024 * 1024
+LATE = 24 * 1024 * 1024
+LAST = LATE
 
 
 def tile_of(size, most):
@@ -64,6 +66,7 @@
         self.steps = phases * chunks
         self.ys, self.xs = 2, n // 4
         self.step = width // chunks
+        self.slots = min(self.steps, 8)
 
     def scratch(self):
         p, y, x, share, width, v = self.phases, self.ys, self.xs, self.share, self.width, self.steps
@@ -79,16 +82,9 @@
             VMEM((p, x, share, width), BF16),
             VMEM((self.kinds, y, x, 2, share, width), BF16),
         ] + [
-            DMA((v,)), DMA((v,)),
-            DMA((v, x)), DMA((v, x)),
-            DMA((v,)), DMA((v,)),
-            DMA((v,)), DMA((v,)),
-            DMA((v, x)), DMA((v, x)),
-            DMA((v, x)), DMA((v, x)),
-            DMA((v,)), DMA((v,)),
-            DMA((v, x)), DMA((v, x)),
-            DMA((v, x)), DMA((v, x)),
-            DMA((v, y * x)), DMA((v, y * x)),
+            DMA(shape)
+            for one, slots in zip((1, x - 1, 1, 1, x - 1, x - 1, 1, x - 1, x - 1, 1), [self.slots] * 9 + [v])
+            for shape in ((one,), (slots, one))
         ]
 
     def bind(self, refs):
@@ -123,33 +119,31 @@
     def row(self, s):
         return self.at(self.py, self.to[s], self.core)
 
+    def copy(self, which, src, dst, v, target, k=1):
+        send, recv = self.sems[which]
+        return remote(src, dst, send.at[k - 1], recv.at[lax.rem(v, recv.shape[0]), k - 1], target)
+
     def mated(self, v):
-        p, cols, (s, r) = self.phase(v), self.cols(v), self.sems[0]
-        return remote(
-            self.x.at[p, :, :, :, 1 - self.core, :, cols], self.mate_in.at[p, :, :, :, :, cols], s.at[v], r.at[v], self.mate
-        )
+        p, cols = self.phase(v), self.cols(v)
+        src = self.x.at[p, :, :, :, 1 - self.core, :, cols]
+        return self.copy(0, src, self.mate_in.at[p, :, :, :, :, cols], v, self.mate)
 
     def first_x(self, v, k):
-        p, cols, (s, r) = self.phase(v), self.cols(v), self.sems[1]
-        return remote(
-            self.paired.at[p, 0, :, self.to[k], :, cols], self.x1.at[p, self.px, :, :, cols], s.at[v, k], r.at[v, k], self.row(k)
-        )
+        p, cols = self.phase(v), self.cols(v)
+        src = self.paired.at[p, 0, :, self.to[k], :, cols]
+        return self.copy(1, src, self.x1.at[p, self.px, :, :, cols], v, self.row(k), k)
 
     def first_y(self, v):
-        p, cols, (s, r) = self.phase(v), self.cols(v), self.sems[2]
-        return remote(
-            self.paired.at[p, 1, self.qy, :, :, cols], self.y1.at[p, :, :, cols], s.at[v], r.at[v], self.across
-        )
+        p, cols = self.phase(v), self.cols(v)
+        return self.copy(2, self.paired.at[p, 1, self.qy, :, :, cols], self.y1.at[p, :, :, cols], v, self.across)
 
     def second_y(self, v):
-        p, cols, (s, r) = self.phase(v), self.cols(v), self.sems[3]
-        return remote(self.sa.at[p, :, cols], self.y2.at[p, :, cols], s.at[v], r.at[v], self.across)
+        p, cols = self.phase(v), self.cols(v)
+        return self.copy(3, self.sa.at[p, :, cols], self.y2.at[p, :, cols], v, self.across)
 
     def second_x(self, v, k):
-        p, cols, (s, r) = self.phase(v), self.cols(v), self.sems[4]
-        return remote(
-            self.sb.at[p, self.to[k], :, cols], self.x2.at[p, self.px, :, cols], s.at[v, k], r.at[v, k], self.row(k)
-        )
+        p, cols = self.phase(v), self.cols(v)
+        return self.copy(4, self.sb.at[p, self.to[k], :, cols], self.x2.at[p, self.px, :, cols], v, self.row(k), k)
 
     def block(self, v, y, x):
         if self.phases > 1:
@@ -157,39 +151,38 @@
         return self.full.at[:, y, x, self.core, :, self.cols(v)]
 
     def half(self, v, y, x, part):
-        if self.phases > 1:
-            parts = 2 if self.step % 256 == 0 else 1
-            if parts == 1:
-                rows = pl.ds(part * (self.share // 2), self.share // 2)
-                return self.full.at[self.phase(v), y, x, self.core, rows, self.cols(v)]
+        if self.phases == 1:
+            return self.full.at[part, y, x, self.core, :, self.cols(v)]
+        if self.step % 256 == 0:
             return self.full.at[self.phase(v), y, x, self.core, :, self.cols(v, part, 2)]
-        return self.full.at[part, y, x, self.core, :, self.cols(v)]
+        rows = pl.ds(part * (self.share // 2), self.share // 2)
+        return self.full.at[self.phase(v), y, x, self.core, rows, self.cols(v)]
 
     def gather_x(self, v, k):
-        s, r = self.sems[5]
         mine = self.block(v, self.py, self.px)
-        return remote(mine, mine, s.at[v, k], r.at[v, k], self.row(k))
+        return self.copy(5, mine, mine, v, self.row(k), k)
 
     def gather_y(self, v):
-        s, r = self.sems[6]
         mine = self.block(v, self.py, self.px)
-        return remote(mine, mine, s.at[v], r.at[v], self.across)
+        return self.copy(6, mine, mine, v, self.across)
 
     def pass_y(self, v, k):
-        s, r = self.sems[7]
         piece = self.half(v, self.py, self.off[k], 0)
-        return remote(piece, piece, s.at[v, k], r.at[v, k], self.across)
+        return self.copy(7, piece, piece, v, self.across, k)
 
     def pass_x(self, v, k):
-        s, r = self.sems[8]
         piece = self.half(v, self.qy, self.px, 1)
-        return remote(piece, piece, s.at[v, k], r.at[v, k], self.row(k))
+        return self.copy(8, piece, piece, v, self.row(k), k)
 
     def hand(self, v, role):
-        s, r = self.sems[9]
         y, k = (self.py, role) if role < self.xs else (self.qy, role - self.xs)
         piece = self.block(v, y, self.off[k])
-        return remote(piece, piece, s.at[v, role], r.at[v, role], self.mate)
+        return self.copy(9, piece, piece, v, self.mate)
+
+    def handed(self, v):
+        kinds = self.phase(v) if self.phases > 1 else slice(None)
+        every = self.full.at[kinds, :, :, self.core, :, self.cols(v)]
+        return self.copy(9, every, every, v, self.mate)
 
     def put(self, v, kind, rows):
         p, cols = self.phase(v), self.cols(v)
@@ -261,28 +254,30 @@
             self.hand(v, self.xs + k).start()
 
     def complete(self, v):
-        for role in range(2 * self.xs):
-            self.hand(v, role).wait_recv()
+        self.handed(v).wait_recv()
 
     def rows(self, v, kind):
         cols = self.cols(v)
         return self.full[kind, :, :, :, :, cols].reshape(self.n * self.share, self.step)
 
     def drain(self):
-        @pl.loop(0, self.steps)
-        def _(v):
-            self.mated(v).wait_send()
-            self.first_y(v).wait_send()
-            self.second_y(v).wait_send()
-            self.gather_y(v).wait_send()
-            for k in range(1, self.xs):
-                for copy in (self.first_x, self.second_x, self.gather_x, self.pass_y, self.pass_x):
-                    copy(v, k).wait_send()
-            for role in range(2 * self.xs):
-                self.hand(v, role).wait_send()
-
-
-LAGS = dict(pair=1, cross=3, totals=5, relay=7, last=9, done=10)
+        full = self.full
+        mine, half = full.at[:, self.py, self.px, self.core], full.at[0, self.py, self.px, self.core]
+        every = full.at[:, :, :, self.core]
+        self.copy(0, self.x.at[:, :, :, :, 1 - self.core], self.mate_in, 0, self.mate).wait_send()
+        self.copy(2, self.paired.at[:, 1, self.qy], self.y1, 0, self.across).wait_send()
+        self.copy(3, self.sa, self.y2, 0, self.across).wait_send()
+        self.copy(6, mine, mine, 0, self.across).wait_send()
+        self.copy(9, every, every, 0, self.mate).wait_send()
+        for k in range(1, self.xs):
+            self.copy(1, self.paired.at[:, 0, :, self.to[k]], self.x1.at[:, self.px], 0, self.row(k), k).wait_send()
+            self.copy(4, self.sb.at[:, self.to[k]], self.x2.at[:, self.px], 0, self.row(k), k).wait_send()
+            self.copy(5, mine, mine, 0, self.row(k), k).wait_send()
+            self.copy(7, half, half, 0, self.across, k).wait_send()
+            self.copy(8, half, half, 0, self.row(k), k).wait_send()
+
+
+LAGS = dict(pair=1, cross=3, unit=3, totals=5, relay=7, last=9, done=10)
 
 
 def staged(i, lag, steps, body):
@@ -371,17 +366,20 @@
             for copy in copies(jnp.int32(c)):
                 copy.start()
 
+    def turn(copies, c, body):
+        for copy in copies(c):
+            copy.wait()
+        body(c, lax.rem(c, SLOTS))
+
+        @pl.when(c + SLOTS < chunks)
+        def _():
+            for copy in copies(c + SLOTS):
+                copy.start()
+
     def run_stream(copies, body):
         @pl.loop(0, chunks)
         def _(c):
-            for copy in copies(c):
-                copy.wait()
-            body(c, lax.rem(c, SLOTS))
-
-            @pl.when(c + SLOTS < chunks)
-            def _():
-                for copy in copies(c + SLOTS):
-                    copy.start()
+            turn(copies, c, body)
 
     gate_stream = functools.partial(wide_copies, along_gate, before_gate)
     up_stream = functools.partial(wide_copies, along_up, before_up)
@@ -404,8 +402,7 @@
         squares(wide.at[slot, 0], wide.at[slot, 1], norms)
 
     run_stream(gate_stream, norm_wide)
-    load_down.start()
-    load_along.start()
+    open_stream(up_stream)
     for i in range(t - 1):
         gather(i).wait_recv()
 
@@ -487,13 +484,36 @@
         for i in range(t - 1):
             z_second(p, i).start()
 
+    def before_of(kind):
+        def body(c, slot):
+            bx[kind, :, col(c)] = dot(everyone(), wide[slot, 1]).astype(BF16)
+
+        return body
+
+    def norm_and_before(c, slot):
+        norm_wide(c, slot)
+        before_of(1)(c, slot)
+
+    def norm_tall(c, slot):
+        squares(tall.at[slot, 0], tall.at[slot, 1], norms)
+
+    def unit(v):
+        @pl.when(v < chunks)
+        def _():
+            turn(up_stream, v, norm_and_before)
+
+        @pl.when(v >= chunks)
+        def _():
+            turn(tall_copies, v - chunks, norm_tall)
+
     ready = chunks - 1 + LAGS["done"]
     last = steps + LAGS["done"]
-    settle = min(ready + 6, last - 1)
+    settle = min(ready + 4, last - 1)
 
     @pl.loop(0, last)
     def _(i):
         staged(i, 0, steps, front)
+        staged(i, LAGS["unit"], steps, unit)
         staged(i, LAGS["cross"], steps, width.cross)
         staged(i, LAGS["totals"], steps, sums)
         staged(i, LAGS["relay"], steps, width.relay)
@@ -501,6 +521,18 @@
         staged(i, LAGS["done"], steps, middle)
         staged(i, LAGS["pair"], steps, width.pair)
 
+        @pl.when(i == min(4, ready))
+        def _():
+            load_down.start()
+
+        @pl.when(i == min(7, ready))
+        def _():
+            open_stream(tall_copies)
+
+        @pl.when(i == min(11, ready))
+        def _():
+            load_along.start()
+
         @pl.when(i == ready)
         def _():
             z_send(0)
@@ -510,17 +542,7 @@
             z_finish(0)
 
     z_send(1)
-    open_stream(up_stream)
-
-    def before_of(kind):
-        def body(c, slot):
-            bx[kind, :, col(c)] = dot(everyone(), wide[slot, 1]).astype(BF16)
-
-        return body
-
-    def norm_and_before(c, slot):
-        norm_wide(c, slot)
-        before_of(1)(c, slot)
+    open_stream(again_stream)
 
     stores = [
         pltpu.make_async_copy(tok, out_tokens, o_sem.at[0]),
@@ -529,18 +551,11 @@
     ]
     for store in stores:
         store.start()
-    run_stream(up_stream, norm_and_before)
-    open_stream(tall_copies)
-    open_stream(again_stream)
-    z_finish(1)
-
-    def norm_tall(c, slot):
-        squares(tall.at[slot, 0], tall.at[slot, 1], norms)
-
-    run_stream(tall_copies, norm_tall)
     run_stream(again_stream, before_of(0))
     stores.append(pltpu.make_async_copy(bx, out_before, o_sem.at[3]))
     stores[-1].start()
+    z_finish(1)
+
     for p in range(2):
         for i in range(t - 1):
             z_second(p, i).wait_recv()
@@ -609,12 +624,11 @@
 
 
 def late_kernel(n, t, entries, width, *refs):
-    (tokens, units, keeps_in, grads_in, before_in, norms, down, along, before, beta_prev) = refs[:10]
-    (out_dirs, scales) = refs[10:12]
-    (grads, hidden, keeps, bx, downs, alongs, befores, sums, gram, swap_gram) = refs[12:22]
-    (dp_in, total_dp, tp_in) = refs[22:25]
-    (in_sem, m_sem, o_sem, s1, r1, s2, r2) = refs[25:32]
-    width.bind(refs[32:])
+    (tokens, units, keeps_in, grads_in, before_in, norms, down, along, before) = refs[:9]
+    wide_in, beta_prev, out_dirs, scales, alongs, wide_out = refs[9:12], refs[12], refs[13], refs[14], refs[15], refs[16:19]
+    (grads, hidden, keeps, bx, downs, befores, sums, gram, swap_gram, dp_in, total_dp, tp_in) = refs[19:31]
+    (in_sem, m_sem, w_sem, o_sem, s1, r1, s2, r2) = refs[31:39]
+    width.bind(refs[39:])
     chunks, steps, step = width.chunks, width.steps, width.step
     depth = down.shape[1]
     rows = n * width.share
@@ -628,24 +642,34 @@
     ]
 
     def matrix(which, c):
-        src, dst = ((down, downs), (along, alongs), (before, befores))[which]
-        at = width.cols(c)
-        return pltpu.make_async_copy(src.at[at, :], dst.at[at, :], m_sem.at[which, c])
-
-    loads[0].start()
-    for c in range(chunks):
-        matrix(0, jnp.int32(c)).start()
-        matrix(1, jnp.int32(c)).start()
-        if c == 0:
-            for load in loads[1:]:
-                load.start()
-    for c in range(chunks):
-        matrix(2, jnp.int32(c)).start()
+        at, slot = width.cols(c), lax.rem(c, DEEP)
+        src = (down, along, before)[which].at[at, :]
+        dst = alongs.at[at, :] if which == 1 else (downs, befores)[which // 2].at[slot]
+        return pltpu.make_async_copy(src, dst, m_sem.at[which, slot])
+
+    def fetch(c):
+        @pl.when(c < steps)
+        def _():
+            for which in range(3):
+                matrix(which, c).start()
+
+    def ahead(c):
+        for src, dst, sem in zip(wide_in, wide_out, range(3)):
+            at = width.cols(c)
+            pltpu.make_async_copy(src.at[:, at], dst.at[:, at], w_sem.at[sem]).start()
+
+    for load in loads:
+        load.start()
+    for c in range(2):
+        fetch(jnp.int32(c))
     sums[...] = jnp.zeros_like(sums)
     gram[...] = jnp.zeros_like(gram)
     swap_gram[...] = jnp.zeros_like(swap_gram)
     greet([{"dp": spot} for spot in dp_spots] + [{"tp": spot} for spot in tp_spots])
-    for load in loads:
+    loads[0].wait()
+    for c in range(2, DEEP - 1):
+        fetch(jnp.int32(c))
+    for load in loads[1:]:
         load.wait()
 
     def both():
@@ -662,16 +686,17 @@
         matrix(0, v).wait()
         matrix(1, v).wait()
         at = width.cols(v)
-        weighted = against(both(), downs[at, :])
+        weighted = against(both(), downs[lax.rem(v, DEEP)])
         moved = against(both(), alongs[at, :])
         width.put(v, 0, weighted[:rows])
         width.put(v, 1, weighted[rows:] + moved[:rows])
         width.mated(v).start()
         crossed(1, v, moved)
+        fetch(v + DEEP - 1)
 
     def extra(v):
         matrix(2, v).wait()
-        crossed(2, v, against(both(), befores[width.cols(v), :]))
+        crossed(2, v, against(both(), befores[lax.rem(v, DEEP)]))
         swapped = jnp.concatenate([unit(v, 1), unit(v, 0)])
         swap_gram[...] += against(swapped, swapped)
 
@@ -702,6 +727,7 @@
 
     @pl.loop(0, steps + LAGS["done"])
     def _(i):
+        staged(i, 1, steps, extra)
         staged(i, 0, steps, back)
         staged(i, LAGS["cross"], steps, width.cross)
         staged(i, LAGS["totals"], steps, middle)
@@ -709,7 +735,7 @@
         staged(i, LAGS["last"], steps, width.relay_last)
         staged(i, LAGS["done"], steps, finish)
         staged(i, LAGS["pair"], steps, width.pair)
-        staged(i, LAGS["totals"], steps, extra)
+        staged(i, 6, steps, ahead)
 
     store = pltpu.make_async_copy(width.full, out_dirs, o_sem.at[0])
     store.start()
@@ -769,9 +795,11 @@
         copy.wait_send()
     width.drain()
     store.wait()
-
-
-def late(n, t, entries, tokens, units, keeps, grads, bx, norms, down, along, before, beta_prev):
+    for src, dst, sem in zip(wide_in, wide_out, range(3)):
+        pltpu.make_async_copy(src, dst, w_sem.at[sem]).wait()
+
+
+def late(n, t, entries, tokens, units, keeps, grads, bx, norms, down, along, before, wides, beta_prev):
     width, depth = down.shape
     rows = bx.shape[1]
     chunks = width // tile_of(width, max(128, width // 8))
@@ -779,17 +807,17 @@
     small = (8, 128)
     return pl.pallas_call(
         functools.partial(late_kernel, n, t, entries, plan),
-        out_shape=[jax.ShapeDtypeStruct(units.shape, BF16), jax.ShapeDtypeStruct(small, F32)],
-        in_specs=[WHOLE] + [ANY] * 4 + [WHOLE] + [ANY] * 3 + [pl.BlockSpec(memory_space=pltpu.SMEM)],
-        out_specs=[ANY, WHOLE],
+        out_shape=[jax.ShapeDtypeStruct(units.shape, BF16), jax.ShapeDtypeStruct(small, F32)]
+        + [VMEM(like.shape, BF16) for like in (along,) + wides],
+        in_specs=[WHOLE] + [ANY] * 4 + [WHOLE] + [ANY] * 6 + [pl.BlockSpec(memory_space=pltpu.SMEM)],
+        out_specs=[ANY] + [WHOLE] * 5,
         scratch_shapes=[
             VMEM(grads.shape, BF16),
             VMEM(units.shape, BF16),
             VMEM(keeps.shape, F32),
             VMEM(bx.shape, BF16),
-            VMEM((width, depth), BF16),
-            VMEM((width, depth), BF16),
-            VMEM((width, depth), BF16),
+            VMEM((DEEP, plan.step, depth), BF16),
+            VMEM((DEEP, plan.step, depth), BF16),
             VMEM((3,) + small, F32),
             VMEM((rows, rows), F32),
             VMEM((2 * rows, 2 * rows), F32),
@@ -797,7 +825,8 @@
             VMEM(small, F32),
             VMEM((t,) + small, F32),
             DMA((4,)),
-            DMA((3, chunks)),
+            DMA((3, DEEP)),
+            DMA((3,)),
             DMA((1,)),
             DMA((n - 1,)),
             DMA((n - 1,)),
@@ -805,52 +834,132 @@
             DMA((t - 1,)),
         ]
         + plan.scratch(),
-        compiler_params=pltpu.CompilerParams(collective_id=2, has_side_effects=True, vmem_limit_bytes=LIMIT),
-    )(tokens, units, keeps, grads, bx, norms, down, along, before, beta_prev)
-
-
-def transposed(one, two):
-    return lax.dot_general(one, two, (((0,), (0,)), ((), ())), preferred_element_type=F32)
-
-
-def next_kernel(scales, tokens, dirs, units, grads, along_gate, along_up, along_down, before_gate, before_up, before_down, out_gate, out_up, out_down, tall):
+        compiler_params=pltpu.CompilerParams(collective_id=2, has_side_effects=True, vmem_limit_bytes=LATE),
+    )(tokens, units, keeps, grads, bx, norms, down, along, before, *wides, beta_prev)
+
+
+def next_kernel(scales, tokens, dirs, units, grads, before_up, before_down, along_down, along_gate, along_up, before_gate, *refs):
+    out_gate, out_up, out_down, coefs, tok, tall, ways, hidden, slopes, ups, downs, wides, talls, in_sem, b_sem, o_sem = refs
     inverse, alpha, beta = scales[2, 0], scales[3, 0], scales[4, 0]
-
-    @pl.when(pl.program_id(0) == 0)
-    def _():
-        tall[...] = tokens[...].T
-
-    def blend(image, along, before, out):
-        out[...] = (image * inverse - along[...].astype(F32) * alpha - before[...].astype(F32) * beta).astype(BF16)
-
-    blend(dot(tall[...], dirs[0]), along_gate, before_gate, out_gate)
-    blend(dot(tall[...], dirs[1]), along_up, before_up, out_up)
-    image = transposed(units[1], grads[0]) + transposed(units[0], grads[1])
-    blend(image, along_down, before_down, out_down)
-
-
-def next_parts(scales, tokens, dirs, units, grads, alongs, befores):
+    depth, width = along_gate.shape
+    rows = tokens.shape[0]
+    tile, part = wides.shape[2], tile_of(depth, 256)
+    count = width // tile
+    loads = [
+        pltpu.make_async_copy(src, dst, in_sem.at[i])
+        for i, (src, dst) in enumerate(
+            ((tokens, tok), (dirs.at[0], ways.at[0]), (dirs.at[1], ways.at[1]), (units, hidden), (grads, slopes))
+        )
+    ]
+    for load in loads:
+        load.start()
+
+    def piece(j):
+        return pl.ds(pl.multiple_of(j * tile, tile), tile)
+
+    def previous(which, j):
+        slot = lax.rem(j, DEEP)
+        src, dst = ((before_up.at[:, piece(j)], ups), (before_down.at[piece(j), :], downs))[which]
+        return pltpu.make_async_copy(src, dst.at[slot], b_sem.at[which, slot])
+
+    for which in range(2):
+        for j in range(min(DEEP, count)):
+            previous(which, jnp.int32(j)).start()
+    coefs[0] = scales[0, 0]
+    coefs[1] = scales[1, 0]
+
+    def blend(image, along, before):
+        return (image * inverse - along.astype(F32) * alpha - before.astype(F32) * beta).astype(BF16)
+
+    def store(which, j):
+        slot = lax.rem(j, DEEP)
+        if which < 2:
+            dst, src = (out_gate, out_up)[which].at[:, piece(j)], wides.at[slot]
+        else:
+            dst, src = out_down.at[piece(j), :], talls.at[slot]
+        return pltpu.make_async_copy(src, dst, o_sem.at[min(which, 2) // 2, slot])
+
+    loads[0].wait()
+    tall[...] = tok[...].T
+    for which, along in enumerate((along_gate, along_up)):
+        loads[1 + which].wait()
+
+        @pl.loop(0, count)
+        def _(j):
+            slot, cols = lax.rem(j, DEEP), piece(j)
+            if which == 0:
+                @pl.when(j >= DEEP)
+                def _():
+                    store(0, j).wait()
+            else:
+                previous(0, j).wait()
+                store(0, j).wait()
+            way = ways[which, :, cols]
+            for at in range(0, depth, part):
+                here = slice(at, at + part)
+                before = ups[slot, here, :] if which else before_gate[here, cols]
+                wides[slot, here, :] = blend(dot(tall[here, :], way), along[here, cols], before)
+            store(which, j).start()
+            if which:
+                @pl.when(j + DEEP < count)
+                def _():
+                    previous(0, j + DEEP).start()
+
+    loads[3].wait()
+    loads[4].wait()
+
+    @pl.loop(0, count)
+    def _(j):
+        slot, cols = lax.rem(j, DEEP), piece(j)
+
+        @pl.when(j >= DEEP)
+        def _():
+            store(2, j).wait()
+
+        previous(1, j).wait()
+        swapped = jnp.concatenate([hidden[1, :, cols], hidden[0, :, cols]]).T
+        for at in range(0, depth, part):
+            here = slice(at, at + part)
+            both = slopes[:, :, here].reshape(2 * rows, part)
+            talls[slot, :, here] = blend(dot(swapped, both), along_down[cols, here], downs[slot, :, here])
+        store(2, j).start()
+
+        @pl.when(j + DEEP < count)
+        def _():
+            previous(1, j + DEEP).start()
+
+    for j in range(min(DEEP, count)):
+        store(0, jnp.int32(j)).wait()
+        store(2, jnp.int32(j)).wait()
+
+
+def next_parts(scales, tokens, dirs, units, grads, before_up, before_down, *held):
     rows, depth = tokens.shape
     width = dirs.shape[2]
-    tile = tile_of(width, 256)
-    wide = pl.BlockSpec((depth, tile), lambda i: (0, i))
-    tall = pl.BlockSpec((tile, depth), lambda i: (i, 0))
+    tile = tile_of(width, max(128, min(256, width // DEEP)))
+    smem = pl.BlockSpec(memory_space=pltpu.SMEM)
     return pl.pallas_call(
         next_kernel,
-        grid=(width // tile,),
-        out_shape=[jax.ShapeDtypeStruct((depth, width), BF16)] * 2 + [jax.ShapeDtypeStruct((width, depth), BF16)],
-        in_specs=[
-            pl.BlockSpec(memory_space=pltpu.SMEM),
-            pl.BlockSpec((rows, depth), lambda i: (0, 0)),
-            pl.BlockSpec((2, rows, tile), lambda i: (0, 0, i)),
-            pl.BlockSpec((2, rows, tile), lambda i: (0, 0, i)),
-            pl.BlockSpec((2, rows, depth), lambda i: (0, 0, 0)),
-        ]
-        + [wide, wide, tall] * 2,
-        out_specs=[wide, wide, tall],
-        scratch_shapes=[VMEM((depth, rows), BF16)],
-        compiler_params=pltpu.CompilerParams(vmem_limit_bytes=LIMIT),
-    )(scales, tokens, dirs, units, grads, *alongs, *befores)
+        out_shape=[jax.ShapeDtypeStruct((depth, width), BF16)] * 2
+        + [jax.ShapeDtypeStruct((width, depth), BF16), jax.ShapeDtypeStruct((2,), F32)],
+        in_specs=[smem] + [ANY] * 6 + [WHOLE] * 4,
+        out_specs=[ANY] * 3 + [smem],
+        scratch_shapes=[
+            VMEM((rows, depth), BF16),
+            VMEM((depth, rows), BF16),
+            VMEM(dirs.shape, BF16),
+            VMEM(dirs.shape, BF16),
+            VMEM(grads.shape, BF16),
+            VMEM((DEEP, depth, tile), BF16),
+            VMEM((DEEP, tile, depth), BF16),
+            VMEM((DEEP, depth, tile), BF16),
+            VMEM((DEEP, tile, depth), BF16),
+            DMA((5,)),
+            DMA((2, DEEP)),
+            DMA((2, DEEP)),
+        ],
+        compiler_params=pltpu.CompilerParams(vmem_limit_bytes=LAST),
+    )(scales, tokens, dirs, units, grads, before_up, before_down, *held)
 
 
 def on_device(
@@ -885,20 +994,22 @@
         previous_down,
     )
     entries = float(n * t * (gate_weight.size + up_weight.size + down_weight.size))
-    dirs, scales = late(
-        n, t, entries, everyone, units, keeps, grads, bx, norms, down_weight, direction_down, previous_down, beta_prev
+    wides = (direction_gate, direction_up, previous_gate)
+    dirs, scales, *held = late(
+        n, t, entries, everyone, units, keeps, grads, bx, norms, down_weight, direction_down, previous_down, wides, beta_prev
     )
+    held = [pltpu.with_memory_space_constraint(array, VMEM) for array in held]
     rows, depth = bx.shape[1], tokens.shape[1]
-    next_gate, next_up, next_down = next_parts(
+    return tuple(next_parts(
         scales,
         everyone.reshape(rows, depth),
         dirs.reshape(bx.shape),
         units.reshape(bx.shape),
         grads.reshape(2, rows, depth),
-        (direction_gate, direction_up, direction_down),
-        (previous_gate, previous_up, previous_down),
-    )
-    return (next_gate, next_up, next_down, scales[:2, 0])
+        previous_up,
+        previous_down,
+        *held,
+    ))
 
 
 def solution(mesh):

time: 170 us -> 141 us (0.83)
  Pallas kernels: 167 us -> 139 us
    pallas_call x1, Pallas kernels: 83.6 us -> 71.6 us  [early(): pl.pallas_call(functools.partial(early_kernel, n, t, plan), out_shape=[ja...]
    pallas_call x1, Pallas kernels: 32 us -> 23 us  [next_parts(): pl.pallas_call(next_kernel, out_shape=[jax.ShapeDtypeStruct((depth, width...]
    pallas_call x1, Pallas kernels: 51.4 us -> 44.3 us  [late(): pl.pallas_call(functools.partial(late_kernel, n, t, entries, plan), out_s...]
where the time goes in v2:
time: 141 us; the launch traced here: 140 us
  Pallas kernels  139 us (99%)
    pallas_call x1, Pallas kernels, early(): pl.pallas_call(functools.partial(early_kernel, n, t, plan), out_shape=[ja...  71.6 us
    pallas_call x1, Pallas kernels, late(): pl.pallas_call(functools.partial(late_kernel, n, t, entries, plan), out_s...  44.3 us
    pallas_call x1, Pallas kernels, next_parts(): pl.pallas_call(next_kernel, out_shape=[jax.ShapeDtypeStruct((depth, width...  23 us

profile of v2, /device:TPU:0, one launch (start us, length us, event | category | flops | bytes accessed | tf_op | source)
XLA Modules:
  0.0 140.2 jit_solution(9126010054092009016)
XLA Ops:
  1.3 71.6 %shard_map.147 = (bf16[4,32,1024]{2,1,0:T(8,128)(2,1)}, bf16[2,2,2,2,16,4096]{5,4,3,2,1,0:T(8,128)(2,1)}, f32[4,16,4096]{2,1,0:T(8,128)}, bf16[2,4,32,1024]{3,2,...) custom-call(bf16[32,1024]{1,0:T(8,128)(2,1)} %refs_0_.1, bf16[32,1024]{1,0:T(8,128)(2,1)} %refs_1_.1, ...), custom_call_target="tpu_custom_call" | custom-call | tf_op jit(solution)/shard_map/pallas_call | solution.py:584
  72.9 44.3 %shard_map.148 = (bf16[2,2,2,2,16,4096]{5,4,3,2,1,0:T(8,128)(2,1)}, f32[8,128]{1,0:T(8,128)}, bf16[4096,1024]{1,0:T(8,128)(2,1)S(1)}, bf16[1024,4096]{1,0:T(8,12...) custom-call(bf16[4,32,1024]{2,1,0:T(8,128)(2,1)} %get-tuple-element.16.refs_0_, ...), custom_call_target="tpu_custom_call" | custom-call | tf_op jit(solution)/shard_map/pallas_call | solution.py:808
  117.2 23.0 %shard_map.149 = (bf16[1024,4096]{1,0:T(8,128)(2,1)}, bf16[1024,4096]{1,0:T(8,128)(2,1)}, bf16[4096,1024]{1,0:T(8,128)(2,1)}, f32[2]{0:T(128)}) custom-call(f32[8,128]{1,0:T(8,128)} %get-tuple-element.22.scales, bf16[128,1024]{1,0:T(8,128)(2,1)} %bitcast.7, bf16[2,128,4096]{2,1,0:T(8,128)(2,1)} %bitcast.6, bf16[2,128,4096]{2,1,0:T(8,128)(2,1)} %bitcast.4, ...), custom_call_target="tpu_custom_call" | custom-call | tf_op jit(solution)/shard_map/pallas_call | solution.py:941

commit v3 on v2

--- a/solution.py
+++ b/solution.py
@@ -15,7 +15,7 @@
 F32 = jnp.float32
 BF16 = jnp.bfloat16
 LIMIT = 62 * 1024 * 1024
-LATE = 24 * 1024 * 1024
+LATE = 22 * 1024 * 1024
 LAST = LATE
 
 
@@ -277,7 +277,8 @@
             self.copy(8, half, half, 0, self.row(k), k).wait_send()
 
 
-LAGS = dict(pair=1, cross=3, unit=3, totals=5, relay=7, last=9, done=10)
+LAGS = dict(pair=1, cross=4, unit=4, totals=7, relay=9, last=11, done=12)
+LATER = dict(pair=1, cross=4, totals=6, relay=8, last=10, done=11)
 
 
 def staged(i, lag, steps, body):
@@ -625,9 +626,10 @@
 
 def late_kernel(n, t, entries, width, *refs):
     (tokens, units, keeps_in, grads_in, before_in, norms, down, along, before) = refs[:9]
-    wide_in, beta_prev, out_dirs, scales, alongs, wide_out = refs[9:12], refs[12], refs[13], refs[14], refs[15], refs[16:19]
-    (grads, hidden, keeps, bx, downs, befores, sums, gram, swap_gram, dp_in, total_dp, tp_in) = refs[19:31]
-    (in_sem, m_sem, w_sem, o_sem, s1, r1, s2, r2) = refs[31:39]
+    wide_in, beta_prev, out_dirs, scales, alongs, wide_out = refs[9:12], refs[12], refs[13], refs[14], refs[18], refs[19:22]
+    tall, hidden, grads = refs[15:18]
+    (keeps, bx, downs, befores, sums, gram, swap_gram, dp_in, total_dp, tp_in) = refs[22:32]
+    (in_sem, m_sem, w_sem, s1, r1, s2, r2) = refs[32:39]
     width.bind(refs[39:])
     chunks, steps, step = width.chunks, width.steps, width.step
     depth = down.shape[1]
@@ -665,6 +667,7 @@
     sums[...] = jnp.zeros_like(sums)
     gram[...] = jnp.zeros_like(gram)
     swap_gram[...] = jnp.zeros_like(swap_gram)
+    tall[...] = tokens[...].reshape(rows, depth).T
     greet([{"dp": spot} for spot in dp_spots] + [{"tp": spot} for spot in tp_spots])
     loads[0].wait()
     for c in range(2, DEEP - 1):
@@ -722,23 +725,22 @@
         cols = width.cols(v)
         for kind in range(2):
             part = width.rows(v, kind)
+            out_dirs[kind, :, cols] = part
             gram[...] += against(part, part)
             sums[2] += lanes(folded(part.astype(F32) * bx[kind, :, cols].astype(F32)))
 
-    @pl.loop(0, steps + LAGS["done"])
+    @pl.loop(0, steps + LATER["done"])
     def _(i):
         staged(i, 1, steps, extra)
         staged(i, 0, steps, back)
-        staged(i, LAGS["cross"], steps, width.cross)
-        staged(i, LAGS["totals"], steps, middle)
-        staged(i, LAGS["relay"], steps, width.relay)
-        staged(i, LAGS["last"], steps, width.relay_last)
-        staged(i, LAGS["done"], steps, finish)
-        staged(i, LAGS["pair"], steps, width.pair)
+        staged(i, LATER["cross"], steps, width.cross)
+        staged(i, LATER["totals"], steps, middle)
+        staged(i, LATER["relay"], steps, width.relay)
+        staged(i, LATER["last"], steps, width.relay_last)
+        staged(i, LATER["done"], steps, finish)
+        staged(i, LATER["pair"], steps, width.pair)
         staged(i, 6, steps, ahead)
 
-    store = pltpu.make_async_copy(width.full, out_dirs, o_sem.at[0])
-    store.start()
     every = tokens[...].reshape(rows, depth)
     sums[0] += lanes(folded(against(every, every) * gram[...])) + lanes(
         folded(against(both(), both()) * swap_gram[...])
@@ -794,7 +796,6 @@
     for copy in first + second:
         copy.wait_send()
     width.drain()
-    store.wait()
     for src, dst, sem in zip(wide_in, wide_out, range(3)):
         pltpu.make_async_copy(src, dst, w_sem.at[sem]).wait()
 
@@ -807,13 +808,11 @@
     small = (8, 128)
     return pl.pallas_call(
         functools.partial(late_kernel, n, t, entries, plan),
-        out_shape=[jax.ShapeDtypeStruct(units.shape, BF16), jax.ShapeDtypeStruct(small, F32)]
-        + [VMEM(like.shape, BF16) for like in (along,) + wides],
+        out_shape=[VMEM(bx.shape, BF16), jax.ShapeDtypeStruct(small, F32), VMEM((depth, rows), BF16)]
+        + [VMEM(like.shape, BF16) for like in (units, grads, along) + wides],
         in_specs=[WHOLE] + [ANY] * 4 + [WHOLE] + [ANY] * 6 + [pl.BlockSpec(memory_space=pltpu.SMEM)],
-        out_specs=[ANY] + [WHOLE] * 5,
+        out_specs=[WHOLE] * 9,
         scratch_shapes=[
-            VMEM(grads.shape, BF16),
-            VMEM(units.shape, BF16),
             VMEM(keeps.shape, F32),
             VMEM(bx.shape, BF16),
             VMEM((DEEP, plan.step, depth), BF16),
@@ -827,7 +826,6 @@
             DMA((4,)),
             DMA((3, DEEP)),
             DMA((3,)),
-            DMA((1,)),
             DMA((n - 1,)),
             DMA((n - 1,)),
             DMA((t - 1,)),
@@ -838,38 +836,33 @@
     )(tokens, units, keeps, grads, bx, norms, down, along, before, *wides, beta_prev)
 
 
-def next_kernel(scales, tokens, dirs, units, grads, before_up, before_down, along_down, along_gate, along_up, before_gate, *refs):
-    out_gate, out_up, out_down, coefs, tok, tall, ways, hidden, slopes, ups, downs, wides, talls, in_sem, b_sem, o_sem = refs
+def next_kernel(scales, before_up, before_down, dirs, tall, units, grads, along_down, along_gate, along_up, before_gate, *refs):
+    out_gate, out_up, out_down, coefs, slopes, ups, downs, wides, talls, b_sem, o_sem = refs
     inverse, alpha, beta = scales[2, 0], scales[3, 0], scales[4, 0]
     depth, width = along_gate.shape
-    rows = tokens.shape[0]
-    tile, part = wides.shape[2], tile_of(depth, 256)
+    rows = dirs.shape[1]
+    tile, part, deep = wides.shape[2], tile_of(depth, 256), downs.shape[0]
     count = width // tile
-    loads = [
-        pltpu.make_async_copy(src, dst, in_sem.at[i])
-        for i, (src, dst) in enumerate(
-            ((tokens, tok), (dirs.at[0], ways.at[0]), (dirs.at[1], ways.at[1]), (units, hidden), (grads, slopes))
-        )
-    ]
-    for load in loads:
-        load.start()
 
     def piece(j):
         return pl.ds(pl.multiple_of(j * tile, tile), tile)
 
     def previous(which, j):
-        slot = lax.rem(j, DEEP)
-        src, dst = ((before_up.at[:, piece(j)], ups), (before_down.at[piece(j), :], downs))[which]
-        return pltpu.make_async_copy(src, dst.at[slot], b_sem.at[which, slot])
-
-    for which in range(2):
-        for j in range(min(DEEP, count)):
-            previous(which, jnp.int32(j)).start()
+        if which == 0:
+            return pltpu.make_async_copy(before_up.at[:, piece(j)], ups.at[:, piece(j)], b_sem.at[0, j])
+        slot = lax.rem(j, deep)
+        return pltpu.make_async_copy(before_down.at[piece(j), :], downs.at[slot], b_sem.at[1, slot])
+
+    for j in range(count):
+        previous(0, jnp.int32(j)).start()
     coefs[0] = scales[0, 0]
     coefs[1] = scales[1, 0]
 
+    def scaled(values):
+        return (values.astype(F32) * inverse).astype(BF16)
+
     def blend(image, along, before):
-        return (image * inverse - along.astype(F32) * alpha - before.astype(F32) * beta).astype(BF16)
+        return (image - along.astype(F32) * alpha - before.astype(F32) * beta).astype(BF16)
 
     def store(which, j):
         slot = lax.rem(j, DEEP)
@@ -877,13 +870,9 @@
             dst, src = (out_gate, out_up)[which].at[:, piece(j)], wides.at[slot]
         else:
             dst, src = out_down.at[piece(j), :], talls.at[slot]
-        return pltpu.make_async_copy(src, dst, o_sem.at[min(which, 2) // 2, slot])
-
-    loads[0].wait()
-    tall[...] = tok[...].T
-    for which, along in enumerate((along_gate, along_up)):
-        loads[1 + which].wait()
-
+        return pltpu.make_async_copy(src, dst, o_sem.at[which // 2, slot])
+
+    for which, (along, before) in enumerate(((along_gate, before_gate), (along_up, ups))):
         @pl.loop(0, count)
         def _(j):
             slot, cols = lax.rem(j, DEEP), piece(j)
@@ -891,75 +880,71 @@
                 @pl.when(j >= DEEP)
                 def _():
                     store(0, j).wait()
+
+                @pl.when(j == count // 2)
+                def _():
+                    for at in range(min(deep, count)):
+                        previous(1, jnp.int32(at)).start()
             else:
                 previous(0, j).wait()
                 store(0, j).wait()
-            way = ways[which, :, cols]
+            way = scaled(dirs[which, :, cols])
             for at in range(0, depth, part):
                 here = slice(at, at + part)
-                before = ups[slot, here, :] if which else before_gate[here, cols]
-                wides[slot, here, :] = blend(dot(tall[here, :], way), along[here, cols], before)
+                wides[slot, here, :] = blend(dot(tall[here, :], way), along[here, cols], before[here, cols])
             store(which, j).start()
-            if which:
-                @pl.when(j + DEEP < count)
-                def _():
-                    previous(0, j + DEEP).start()
-
-    loads[3].wait()
-    loads[4].wait()
+
+    slopes[...] = scaled(grads[...].reshape(2 * rows, depth))
 
     @pl.loop(0, count)
     def _(j):
         slot, cols = lax.rem(j, DEEP), piece(j)
+        place = lax.rem(j, deep)
 
         @pl.when(j >= DEEP)
         def _():
             store(2, j).wait()
 
         previous(1, j).wait()
-        swapped = jnp.concatenate([hidden[1, :, cols], hidden[0, :, cols]]).T
+        swapped = jnp.concatenate([units[k, :, :, :, :, cols].reshape(rows, tile) for k in (1, 0)]).T
         for at in range(0, depth, part):
             here = slice(at, at + part)
-            both = slopes[:, :, here].reshape(2 * rows, part)
-            talls[slot, :, here] = blend(dot(swapped, both), along_down[cols, here], downs[slot, :, here])
+            talls[slot, :, here] = blend(dot(swapped, slopes[:, here]), along_down[cols, here], downs[place, :, here])
         store(2, j).start()
 
-        @pl.when(j + DEEP < count)
-        def _():
-            previous(1, j + DEEP).start()
+        @pl.when(j + deep < count)
+        def _():
+            previous(1, j + deep).start()
 
     for j in range(min(DEEP, count)):
         store(0, jnp.int32(j)).wait()
         store(2, jnp.int32(j)).wait()
 
 
-def next_parts(scales, tokens, dirs, units, grads, before_up, before_down, *held):
-    rows, depth = tokens.shape
-    width = dirs.shape[2]
+def next_parts(scales, before_up, before_down, *held):
+    depth, width = before_up.shape
+    rows = held[0].shape[1]
     tile = tile_of(width, max(128, min(256, width // DEEP)))
     smem = pl.BlockSpec(memory_space=pltpu.SMEM)
+    count = width // tile
+    deep = min(2 * DEEP, count)
     return pl.pallas_call(
         next_kernel,
         out_shape=[jax.ShapeDtypeStruct((depth, width), BF16)] * 2
         + [jax.ShapeDtypeStruct((width, depth), BF16), jax.ShapeDtypeStruct((2,), F32)],
-        in_specs=[smem] + [ANY] * 6 + [WHOLE] * 4,
+        in_specs=[smem] + [ANY] * 2 + [WHOLE] * len(held),
         out_specs=[ANY] * 3 + [smem],
         scratch_shapes=[
-            VMEM((rows, depth), BF16),
-            VMEM((depth, rows), BF16),
-            VMEM(dirs.shape, BF16),
-            VMEM(dirs.shape, BF16),
-            VMEM(grads.shape, BF16),
+            VMEM((2 * rows, depth), BF16),
+            VMEM((depth, width), BF16),
+            VMEM((deep, tile, depth), BF16),
             VMEM((DEEP, depth, tile), BF16),
             VMEM((DEEP, tile, depth), BF16),
-            VMEM((DEEP, depth, tile), BF16),
-            VMEM((DEEP, tile, depth), BF16),
-            DMA((5,)),
-            DMA((2, DEEP)),
+            DMA((2, count)),
             DMA((2, DEEP)),
         ],
         compiler_params=pltpu.CompilerParams(vmem_limit_bytes=LAST),
-    )(scales, tokens, dirs, units, grads, before_up, before_down, *held)
+    )(scales, before_up, before_down, *held)
 
 
 def on_device(
@@ -998,18 +983,8 @@
     dirs, scales, *held = late(
         n, t, entries, everyone, units, keeps, grads, bx, norms, down_weight, direction_down, previous_down, wides, beta_prev
     )
-    held = [pltpu.with_memory_space_constraint(array, VMEM) for array in held]
-    rows, depth = bx.shape[1], tokens.shape[1]
-    return tuple(next_parts(
-        scales,
-        everyone.reshape(rows, depth),
-        dirs.reshape(bx.shape),
-        units.reshape(bx.shape),
-        grads.reshape(2, rows, depth),
-        previous_up,
-        previous_down,
-        *held,
-    ))
+    held = [pltpu.with_memory_space_constraint(array, VMEM) for array in [dirs] + held]
+    return tuple(next_parts(scales, previous_up, previous_down, *held))
 
 
 def solution(mesh):

time: 141 us -> 135 us (0.957)
  Pallas kernels: 139 us -> 134 us
    pallas_call x1, Pallas kernels: 23 us -> 19.4 us  [next_parts(): pl.pallas_call(next_kernel, out_shape=[jax.ShapeDtypeStruct((depth, width...]
where the time goes in v3:
time: 135 us
  Pallas kernels  134 us (99%)
    pallas_call x1, Pallas kernels, early(): pl.pallas_call(functools.partial(early_kernel, n, t, plan), out_shape=[ja...  70.9 us
    pallas_call x1, Pallas kernels, late(): pl.pallas_call(functools.partial(late_kernel, n, t, entries, plan), out_s...  43.5 us
    pallas_call x1, Pallas kernels, next_parts(): pl.pallas_call(next_kernel, out_shape=[jax.ShapeDtypeStruct((depth, width...  19.4 us

profile of v3, /device:TPU:0, one launch (start us, length us, event | category | flops | bytes accessed | tf_op | source)
XLA Modules:
  0.0 135.1 jit_solution(14542898749517921392)
XLA Ops:
  1.3 70.9 %shard_map.147 = (bf16[4,32,1024]{2,1,0:T(8,128)(2,1)}, bf16[2,2,2,2,16,4096]{5,4,3,2,1,0:T(8,128)(2,1)}, f32[4,16,4096]{2,1,0:T(8,128)}, bf16[2,4,32,1024]{3,2,...) custom-call(bf16[32,1024]{1,0:T(8,128)(2,1)} %refs_0_.1, bf16[32,1024]{1,0:T(8,128)(2,1)} %refs_1_.1, ...), custom_call_target="tpu_custom_call" | custom-call | tf_op jit(solution)/shard_map/pallas_call | solution.py:585
  72.2 43.5 %shard_map.148 = (bf16[2,128,4096]{2,1,0:T(8,128)(2,1)S(1)}, f32[8,128]{1,0:T(8,128)}, bf16[1024,128]{1,0:T(8,128)(2,1)S(1)}, bf16[2,2,2,2,16,4096]{5,4,3,2,1,0:...) custom-call(bf16[4,32,1024]{2,1,0:T(8,128)(2,1)} %get-tuple-element., ...), custom_call_target="tpu_custom_call" | custom-call | tf_op jit(solution)/shard_map/pallas_call | solution.py:809
  115.7 19.4 %shard_map.149 = (bf16[1024,4096]{1,0:T(8,128)(2,1)}, bf16[1024,4096]{1,0:T(8,128)(2,1)}, bf16[4096,1024]{1,0:T(8,128)(2,1)}, f32[2]{0:T(128)}) custom-call(f32[8,128]{1,0:T(8,128)} %get-tuple-element.25.scales, bf16[1024,4096]{1,0:T(8,128)(2,1)} %before_up.1, bf16[4096,1024]{1,0:T(8,128)(2,1)} %before_down.1, ...), custom_call_target="tpu_custom_call" | custom-call | tf_op jit(solution)/shard_map/pallas_call | solution.py:931

commit v4 on v3

--- a/solution.py
+++ b/solution.py
@@ -628,15 +628,18 @@
     (tokens, units, keeps_in, grads_in, before_in, norms, down, along, before) = refs[:9]
     wide_in, beta_prev, out_dirs, scales, alongs, wide_out = refs[9:12], refs[12], refs[13], refs[14], refs[18], refs[19:22]
     tall, hidden, grads = refs[15:18]
-    (keeps, bx, downs, befores, sums, gram, swap_gram, dp_in, total_dp, tp_in) = refs[22:32]
-    (in_sem, m_sem, w_sem, s1, r1, s2, r2) = refs[32:39]
-    width.bind(refs[39:])
+    (keeps, bx, downs, befores, sums, gram, swap_gram, mine, box) = refs[22:31]
+    (in_sem, m_sem, w_sem, s1, r1) = refs[31:36]
+    width.bind(refs[36:])
     chunks, steps, step = width.chunks, width.steps, width.step
     depth = down.shape[1]
     rows = n * width.share
     dp, tp = lax.axis_index("dp"), lax.axis_index("tp")
-    dp_spots = [lax.rem(dp + s, n) for s in range(1, n)]
-    tp_spots = [lax.rem(tp + s, t) for s in range(1, t)]
+    everyone, place = n * t, dp * t + tp
+
+    def peer(i):
+        at = lax.rem(place + i, everyone)
+        return {"dp": lax.div(at, t), "tp": lax.rem(at, t)}
 
     loads = [
         pltpu.make_async_copy(src, dst, in_sem.at[i])
@@ -668,7 +671,13 @@
     gram[...] = jnp.zeros_like(gram)
     swap_gram[...] = jnp.zeros_like(swap_gram)
     tall[...] = tokens[...].reshape(rows, depth).T
-    greet([{"dp": spot} for spot in dp_spots] + [{"tp": spot} for spot in tp_spots])
+    barrier = pltpu.get_barrier_semaphore()
+
+    @pl.loop(1, everyone)
+    def _(i):
+        pl.semaphore_signal(barrier, inc=1, device_id=peer(i), device_id_type=MESH)
+
+    pl.semaphore_wait(barrier, everyone - 1)
     loads[0].wait()
     for c in range(2, DEEP - 1):
         fetch(jnp.int32(c))
@@ -745,36 +754,25 @@
     sums[0] += lanes(folded(against(every, every) * gram[...])) + lanes(
         folded(against(both(), both()) * swap_gram[...])
     )
-    shape = (1, 128)
-    own = [jnp.full(shape, jnp.sum(sums[k])) for k in range(3)] + [jnp.full(shape, jnp.sum(norms[k])) for k in range(3)]
+    own = [jnp.sum(sums[k]) for k in range(3)] + [jnp.sum(norms[k]) for k in range(3)]
+    lane = lax.broadcasted_iota(jnp.int32, (1, 128), 1)
+    row = jnp.zeros((1, 128), F32)
     for k in range(6):
-        total_dp[k : k + 1] = own[k]
-    total_dp[6:8] = jnp.zeros((2, 128), F32)
-    dp_in[dp] = total_dp[...]
-
-    first = [
-        remote(total_dp, dp_in.at[dp], s1.at[i], r1.at[i], {"dp": spot}) for i, spot in enumerate(dp_spots)
-    ]
-    for copy in first:
-        copy.start()
-    for copy in first:
-        copy.wait_recv()
-    total = dp_in[0]
-    for at in range(1, n):
-        total = total + dp_in[at]
-    tp_in[tp] = total
-    second = [
-        remote(tp_in.at[tp], tp_in.at[tp], s2.at[i], r2.at[i], {"tp": spot}) for i, spot in enumerate(tp_spots)
-    ]
-    for copy in second:
-        copy.start()
-    for copy in second:
-        copy.wait_recv()
-    total = tp_in[0]
-    for at in range(1, t):
-        total = total + tp_in[at]
-    image_image, image_along, image_before = total[0:1], total[1:2], total[2:3]
-    along_along, along_before, before_before = total[3:4], total[4:5], total[5:6]
+        row = jnp.where(lane == k, own[k], row)
+    mine[...] = row
+
+    @pl.loop(1, everyone)
+    def _(i):
+        remote(mine, box.at[place], s1.at[0], r1.at[0], peer(i)).start()
+
+    box[place] = row
+    others = box.at[pl.ds(0, everyone - 1)]
+    arrivals = remote(others, others, s1.at[0], r1.at[0], peer(1))
+    arrivals.wait_recv()
+    total = box[...].sum(axis=0)
+    image_image, image_along, image_before, along_along, along_before, before_before = (
+        jnp.broadcast_to(total[:, k : k + 1], (1, 128)) for k in range(6)
+    )
     beta_old = beta_prev[0]
     alpha_coef = image_along / entries
     square = (
@@ -793,8 +791,7 @@
     scales[3:4] = alpha_coef * inverse
     scales[4:5] = beta_old * inverse
     scales[5:8] = jnp.zeros((3, 128), F32)
-    for copy in first + second:
-        copy.wait_send()
+    arrivals.wait_send()
     width.drain()
     for src, dst, sem in zip(wide_in, wide_out, range(3)):
         pltpu.make_async_copy(src, dst, w_sem.at[sem]).wait()
@@ -820,16 +817,13 @@
             VMEM((3,) + small, F32),
             VMEM((rows, rows), F32),
             VMEM((2 * rows, 2 * rows), F32),
-            VMEM((n,) + small, F32),
-            VMEM(small, F32),
-            VMEM((t,) + small, F32),
+            VMEM((1, 128), F32),
+            VMEM((n * t, 1, 128), F32),
             DMA((4,)),
             DMA((3, DEEP)),
             DMA((3,)),
-            DMA((n - 1,)),
-            DMA((n - 1,)),
-            DMA((t - 1,)),
-            DMA((t - 1,)),
+            DMA((1,)),
+            DMA((1,)),
         ]
         + plan.scratch(),
         compiler_params=pltpu.CompilerParams(collective_id=2, has_side_effects=True, vmem_limit_bytes=LATE),

time: 135 us -> 133 us (0.985)
  Pallas kernels: 134 us -> 131 us
    pallas_call x1, Pallas kernels: 43.5 us -> 41.1 us  [late(): pl.pallas_call(functools.partial(late_kernel, n, t, entries, plan), out_s...]
where the time goes in v4:
time: 133 us
  Pallas kernels  131 us (98%)
    pallas_call x1, Pallas kernels, early(): pl.pallas_call(functools.partial(early_kernel, n, t, plan), out_shape=[ja...  70.9 us
    pallas_call x1, Pallas kernels, late(): pl.pallas_call(functools.partial(late_kernel, n, t, entries, plan), out_s...  41.1 us
    pallas_call x1, Pallas kernels, next_parts(): pl.pallas_call(next_kernel, out_shape=[jax.ShapeDtypeStruct((depth, width...  19.4 us

profile of v4, /device:TPU:0, one launch (start us, length us, event | category | flops | bytes accessed | tf_op | source)
XLA Modules:
  0.0 132.8 jit_solution(7040330435015692206)
XLA Ops:
  1.3 70.9 %shard_map.147 = (bf16[4,32,1024]{2,1,0:T(8,128)(2,1)}, bf16[2,2,2,2,16,4096]{5,4,3,2,1,0:T(8,128)(2,1)}, f32[4,16,4096]{2,1,0:T(8,128)}, bf16[2,4,32,1024]{3,2,...) custom-call(bf16[32,1024]{1,0:T(8,128)(2,1)} %refs_0_.1, bf16[32,1024]{1,0:T(8,128)(2,1)} %refs_1_.1, ...), custom_call_target="tpu_custom_call" | custom-call | tf_op jit(solution)/shard_map/pallas_call | solution.py:585
  72.2 41.1 %shard_map.148 = (bf16[2,128,4096]{2,1,0:T(8,128)(2,1)S(1)}, f32[8,128]{1,0:T(8,128)}, bf16[1024,128]{1,0:T(8,128)(2,1)S(1)}, bf16[2,2,2,2,16,4096]{5,4,3,2,1,0:...) custom-call(bf16[4,32,1024]{2,1,0:T(8,128)(2,1)} %get-tuple-element., ...), custom_call_target="tpu_custom_call" | custom-call | tf_op jit(solution)/shard_map/pallas_call | solution.py:806
  113.3 19.4 %shard_map.149 = (bf16[1024,4096]{1,0:T(8,128)(2,1)}, bf16[1024,4096]{1,0:T(8,128)(2,1)}, bf16[4096,1024]{1,0:T(8,128)(2,1)}, f32[2]{0:T(128)}) custom-call(f32[8,128]{1,0:T(8,128)} %get-tuple-element.25.scales, bf16[1024,4096]{1,0:T(8,128)(2,1)} %before_up.1, bf16[4096,1024]{1,0:T(8,128)(2,1)} %before_down.1, ...), custom_call_target="tpu_custom_call" | custom-call | tf_op jit(solution)/shard_map/pallas_call | solution.py:925
